TPU v7x, 128 devices: a whole 4x4x4 slice. The times are simulated.
128 devices in a mesh: gx: 16 (over y_lo, x, core), yz: 8 (over z, y_hi).
Axes of the slice: x: 4, y: 4 (y_hi: 2, y_lo: 2; y = y_hi * 2 + y_lo), z: 4, core: 2. Of those that a mesh axis runs over, the one named last changes fastest.
Arguments:
- vel: float32 [3, 96, 192, 1024], P(None, 'gx', 'yz'), may hold values from -6 to 6
- q_old: float32 [3, 96, 192, 1024], P(None, 'gx', None, 'yz'), may hold values from -6 to 6
- pressure_guess: float32 [96, 192, 1024], P('gx', None, 'yz'), may hold values from -6 to 6
- shear_shift: int32 [1], replicated, may hold values from 0 to 1023
Outputs:
- vel_next: float32 [3, 96, 192, 1024], P(None, 'gx', 'yz')
- q_next: float32 [3, 96, 192, 1024], P(None, 'gx', None, 'yz')
- pressure: float32 [96, 192, 1024], P('gx', None, 'yz')
All inputs are finite; a program needn't handle non-finite values.
Results may differ from a plain program's by a relative error of at most 0.00013.
Values sent between devices are 32-bit elements; how exact they have to be, the bound alone decides.
A program may use at most 128 MiB of HBM per device.

v0:
```python
import math

import jax
import jax.numpy as jnp
from jax import lax
from jax.sharding import Mesh
from jax.sharding import PartitionSpec as P

SWEEPS = 2
YZ = ("yz_0", "yz_1")


highest = lax.Precision.HIGHEST
viscosity = 0.05
time_step = 0.2
keep_weight = -5.0 / 9.0
section_weight = 15.0 / 16.0
shear_param = 1.5
fraction = 0.375


def padded_2(cells, sides, width):
    for axis, dim in sides:
        count = lax.axis_size(axis)
        head = lax.slice_in_dim(cells, 0, width, axis=dim)
        tail = lax.slice_in_dim(cells, cells.shape[dim] - width, cells.shape[dim], axis=dim)
        cells = jnp.concatenate(
            [
                lax.ppermute(tail, axis, [(i, (i + 1) % count) for i in range(count)]),
                cells,
                lax.ppermute(head, axis, [((i + 1) % count, i) for i in range(count)]),
            ],
            axis=dim,
        )
    return cells


def in_blocks(shard, dim, devices):
    lengths = shard.shape
    parts = shard.reshape(*lengths[:dim], devices, lengths[dim] // devices, *lengths[dim + 1 :])
    return jnp.moveaxis(parts, dim, 0)


def joined_along(parts, dim):
    lengths = list(parts.shape[1:])
    lengths[dim] *= parts.shape[0]
    return jnp.moveaxis(parts, 0, dim).reshape(lengths)


def exchange_in_order(parts, axes, order):
    inside = parts.shape[1:]
    out = parts.reshape(*(lax.axis_size(a) for a in axes), *inside)
    for k in order:
        out = lax.all_to_all(out, axes[k], k, k, tiled=True)
    return out.reshape(-1, *inside)


def exchange_by_axis(shard, axes, order, split_dim, concat_dim):
    parts = in_blocks(shard, split_dim, lax.axis_size(axes))
    return joined_along(exchange_in_order(parts, axes, order), concat_dim)


def split_parts(packed, block_len):
    shaped = packed.reshape(packed.shape[:-1] + (packed.shape[-1] // (2 * block_len), 2, block_len))
    return (shaped[..., 0:1, :], shaped[..., 1:2, :])


def join_parts(real_part, imag_part, shape):
    return jnp.concatenate([real_part, imag_part], axis=-2).reshape(shape)


def turn(packed, wave, block_len):
    real_part, imag_part = split_parts(packed, block_len)
    return join_parts(-wave * imag_part, wave * real_part, packed.shape)


def scale_modes(packed, factor, block_len):
    real_part, imag_part = split_parts(packed, block_len)
    return join_parts(factor * real_part, factor * imag_part, packed.shape)


def rotate(packed, cosine, sine, block_len):
    real_part, imag_part = split_parts(packed, block_len)
    return join_parts(
        real_part * cosine - imag_part * sine, real_part * sine + imag_part * cosine, packed.shape
    )


def z_apply(packed, cos_z, sin_z, block_len, sign):
    with_cos = jnp.einsum("wz,nxzk->nxwk", cos_z, packed, precision=highest)
    with_sin = jnp.einsum("wz,nxzk->nxwk", sin_z, packed, precision=highest)
    real_part = with_cos[..., :block_len] + sign * with_sin[..., block_len:]
    imag_part = with_cos[..., block_len:] - sign * with_sin[..., :block_len]
    return jnp.concatenate([real_part, imag_part], axis=-1)


def x_slice(padded, offset, rows_x):
    return padded[:, 3 + offset : 3 + offset + rows_x]


def first_diff(padded, rows_x):
    return (
        45.0 * (x_slice(padded, 1, rows_x) - x_slice(padded, -1, rows_x))
        - 9.0 * (x_slice(padded, 2, rows_x) - x_slice(padded, -2, rows_x))
        + (x_slice(padded, 3, rows_x) - x_slice(padded, -3, rows_x))
    ) / 60.0


def second_diff(padded, rows_x):
    return (
        2.0 * (x_slice(padded, 3, rows_x) + x_slice(padded, -3, rows_x))
        - 27.0 * (x_slice(padded, 2, rows_x) + x_slice(padded, -2, rows_x))
        + 270.0 * (x_slice(padded, 1, rows_x) + x_slice(padded, -1, rows_x))
        - 490.0 * x_slice(padded, 0, rows_x)
    ) / 180.0


def local(vel, q_old, pressure_guess, shear_shift):
    rows_x = vel.shape[1]
    width_y = vel.shape[3]
    depth_z = q_old.shape[2]
    groups = lax.axis_size(YZ)
    block_len = width_y // (2 * groups)
    group_id = lax.axis_index(YZ)
    slab_id = lax.axis_index("gx")
    slabs = lax.axis_size("gx")
    total_x = rows_x * slabs
    offset = shear_shift[0]
    padded = padded_2(vel, (("gx", 1),), 3)
    tail_rows = padded[:, :3]
    front_rows = padded[:, rows_x + 3 :]
    moved_tail = (1.0 - fraction) * jnp.roll(tail_rows, -offset, axis=3) + fraction * jnp.roll(
        tail_rows, -offset - 1, axis=3
    )
    moved_front = (1.0 - fraction) * jnp.roll(front_rows, offset, axis=3) + fraction * jnp.roll(
        front_rows, offset + 1, axis=3
    )
    tail_rows = jnp.where(slab_id == 0, moved_tail, tail_rows)
    front_rows = jnp.where(slab_id == slabs - 1, moved_front, front_rows)
    padded = jnp.concatenate([tail_rows, vel, front_rows], axis=1)
    omega = 2.0 / total_x
    xpos = (
        (slab_id * rows_x + jnp.arange(rows_x, dtype=jnp.int32)).astype(jnp.float32)
        + 0.5
        - total_x / 2.0
    )
    background = (-shear_param * omega * xpos)[:, None, None]
    coriolis = jnp.stack(
        [2.0 * omega * vel[1], -(2.0 - shear_param) * omega * vel[0], jnp.zeros_like(vel[0])]
    )
    term_a = (
        -first_diff(padded * padded[0][None], rows_x)
        + viscosity * second_diff(padded, rows_x)
        + coriolis
    )
    term_b = -(vel[1] + background)[None] * vel
    term_c = -vel[2][None] * vel
    columns = jnp.arange(width_y, dtype=jnp.int32)
    part_id = columns // block_len % 2
    mode_col = columns // (2 * block_len) * block_len + columns % block_len
    angle_y = (
        2.0
        * math.pi
        / width_y
        * (columns[:, None] * mode_col[None, :] % width_y).astype(jnp.float32)
    )
    forward_y = jnp.where(part_id[None, :] == 0, jnp.cos(angle_y), -jnp.sin(angle_y)) / math.sqrt(
        width_y
    )

    def to_modes(field):
        flat = field.reshape(-1, width_y)
        return jnp.dot(
            flat, forward_y, precision=highest, preferred_element_type=jnp.float32
        ).reshape(field.shape)

    spec_a = to_modes(term_a)
    spec_b = to_modes(term_b)
    spec_c = to_modes(term_c)
    spec_u = to_modes(vel)
    cells_z = jnp.arange(depth_z, dtype=jnp.int32)
    angle_z = (
        2.0
        * math.pi
        / depth_z
        * (cells_z[:, None] * cells_z[None, :] % depth_z).astype(jnp.float32)
    )
    cos_z = jnp.cos(angle_z) / math.sqrt(depth_z)
    sin_z = jnp.sin(angle_z) / math.sqrt(depth_z)
    signed_z = jnp.where(cells_z < depth_z // 2, cells_z, cells_z - depth_z)
    wave_z = (2.0 * math.pi / depth_z * signed_z.astype(jnp.float32)).reshape(depth_z, 1, 1, 1)
    own_modes = group_id * block_len + jnp.arange(block_len, dtype=jnp.int32)
    own_wave = (2.0 * math.pi / width_y * own_modes.astype(jnp.float32)).reshape(1, 1, block_len)
    all_wave = (
        2.0
        * math.pi
        / width_y
        * jnp.arange(groups * block_len, dtype=jnp.int32).astype(jnp.float32)
    ).reshape(groups, 1, block_len)
    combined = (
        spec_a
        + turn(spec_b, all_wave, block_len)
        - viscosity * scale_modes(spec_u, all_wave * all_wave, block_len)
    )
    spectral = z_apply(exchange_by_axis(combined, YZ, (0, 1), 3, 2), cos_z, sin_z, block_len, 1.0)
    spectral = spectral + turn(
        z_apply(exchange_by_axis(spec_c, YZ, (0, 1), 3, 2), cos_z, sin_z, block_len, 1.0),
        wave_z,
        block_len,
    )
    tendency = spectral - viscosity * scale_modes(
        z_apply(exchange_by_axis(spec_u, YZ, (0, 1), 3, 2), cos_z, sin_z, block_len, 1.0),
        wave_z * wave_z,
        block_len,
    )
    edge_angle = (
        2.0
        * math.pi
        / width_y
        * (
            (own_modes * offset % width_y).astype(jnp.float32)
            + fraction * own_modes.astype(jnp.float32)
        )
    )
    edge_cos = jnp.cos(edge_angle).reshape(1, 1, block_len)
    edge_sin = jnp.sin(edge_angle).reshape(1, 1, block_len)
    denom_half = (
        2.0
        + own_wave.reshape(1, block_len) * own_wave.reshape(1, block_len)
        + wave_z.reshape(depth_z, 1) * wave_z.reshape(depth_z, 1)
    )
    denom = jnp.concatenate([denom_half, denom_half], axis=-1)
    depth_x = SWEEPS + 1
    stacked = jnp.stack([tendency[0], tendency[1], tendency[2], pressure_guess])
    fix_stacked = padded_2(stacked, (("gx", 1),), depth_x)
    extent = fix_stacked.shape[1]
    lower = fix_stacked[:, :depth_x]
    upper = fix_stacked[:, extent - depth_x :]
    middle = fix_stacked[:, depth_x : extent - depth_x]
    lower = jnp.where(slab_id == 0, rotate(lower, edge_cos, edge_sin, block_len), lower)
    upper = jnp.where(slab_id == slabs - 1, rotate(upper, edge_cos, -edge_sin, block_len), upper)
    wide = jnp.concatenate([lower, middle, upper], axis=1)
    along_x = wide[0]
    diverge = (
        0.5 * (along_x[2:] - along_x[:-2])
        + turn(wide[1][1:-1], own_wave, block_len)
        + turn(wide[2][1:-1], wave_z, block_len)
    )
    press = wide[3]
    for sweep_no in range(SWEEPS):
        span_x = press.shape[0] - 2
        press = (press[2:] + press[:-2] - diverge[sweep_no : sweep_no + span_x]) / denom
    slope_x = 0.5 * (press[2:] - press[:-2])
    press = press[1:-1]
    gradient = jnp.stack(
        [slope_x, turn(press, own_wave, block_len), turn(press, wave_z, block_len)]
    )
    q_next = keep_weight * q_old + time_step * (tendency - gradient)
    spatial = z_apply(q_next, cos_z, sin_z, block_len, -1.0)
    weights = jnp.where(mode_col == 0, 1.0, 2.0).astype(jnp.float32)
    inverse_y = (
        jnp.where(part_id[:, None] == 0, jnp.cos(angle_y.T), -jnp.sin(angle_y.T))
        * weights[:, None]
        / math.sqrt(width_y)
    )
    piece = lax.all_to_all(spatial, YZ, split_axis=2, concat_axis=3, tiled=True)
    flat = piece.reshape(-1, width_y)
    correction = jnp.dot(
        flat, inverse_y, precision=highest, preferred_element_type=jnp.float32
    ).reshape(piece.shape)
    vel_next = vel + section_weight * correction
    return (vel_next, q_next, press)


def solution(mesh):
    torus = Mesh(mesh.devices.reshape(mesh.shape["gx"], 4, 2), ("gx", "yz_0", "yz_1"))
    in_specs = (P(None, "gx", YZ, None), P(None, "gx", None, YZ), P("gx", None, YZ), P())
    out_specs = (P(None, "gx", YZ, None), P(None, "gx", None, YZ), P("gx", None, YZ))
    return jax.shard_map(local, mesh=torus, in_specs=in_specs, out_specs=out_specs, check_vma=False)
```

profile of v0, /device:TPU:0, one launch (start us, length us, event | category | flops | bytes accessed | tf_op | source)
XLA Modules:
  0.0 455.0 jit_solution(7538949068420478610)
XLA Ops:
  0.6 3.0 fusion.315
  3.6 3.9 collective-permute-start.1
  9.1 29.9 %fusion.14 = f32[3,6,24,8,128]{4,2,3,1,0:T(8,128)S(1)} fusion(s32[8,128]{1,0:T(8,128)S(1)} %fusion.224, pred[8,128]{1,0:T(8,128)(4,1)S(1)} %fusion.222, f32[3,6,24,1024,1]{3,2,4,1,0:T(8,128)S(1)} %fusion.347), kind=kOutput, calls=%fused_computation.27 | convolution fusion | flops 5453643776 | bytes 3544064 | tf_op jit(solution)/shard_map/dot_general | solution.py:173
  40.3 5.6 %all-to-all-start.2 = ((f32[4,2,3,6,24,128]{5,4,1,3,2,0:T(8,128)}), f32[4,2,3,6,24,128]{5,4,1,3,2,0:T(8,128)}, u32[]{:S(2)}, u32[]{:S(2)}) async-start(f32[4,2,3,6,24,128]{5,4,1,3,2,0:T(8,128)} %copy.58), calls=%async_computation.2 | async-start | bytes 3538944 | tf_op jit(solution)/shard_map/all_to_all | solution.py:54
  49.3 23.8 %fusion.79 = f32[1024,432]{0,1:T(8,128)} fusion(f32[432,1024]{1,0:T(8,128)S(1)} %bitcast.193, s32[1024]{0:T(1024)S(1)} %fusion.220, pred[1024]{0:T(1024)(128)(4,1)S(1)} %fusion.217), kind=kOutput, calls=%fused_computation.99 | convolution fusion | flops 5453643776 | bytes 3544064 | tf_op jit(solution)/shard_map/dot_general | solution.py:173
  73.0 4.8 %reshape_reshape.4 = f32[3,6,24,8,2,64]{5,4,3,2,1,0:T(2,128)} reshape(f32[432,1024]{1,0:T(8,128)} %bitcast.209) | data formatting | bytes 3538944 | tf_op jit(solution)/shard_map/reshape;reshape | solution.py:64
  77.9 8.8 %slice_multiply_fusion.3 = (f32[3,6,24,8,1,64]{5,4,3,2,1,0:T(1,128)}, f32[3,6,24,8,1,64]{5,4,3,2,1,0:T(1,128)}) fusion(f32[3,6,24,8,2,64]{5,4,3,2,1,0:T(2,128)} %reshape_reshape.4, f32[8,64]{1,0:T(8,128)S(1)} %fusion.232), kind=kLoop, calls=%fused_computation.126 | loop fusion | flops 442368 | bytes 3540992 | tf_op jit(solution)/shard_map/mul | solution.py:79
  86.6 42.1 %fusion.16 = f32[3,6,24,8,2,64]{5,2,4,3,1,0:T(8,128)S(1)} fusion(s32[8,2,64]{2,1,0:T(2,128)S(1)} %fusion.207, pred[8,2,64]{2,1,0:T(4,128)(4,1)S(1)} %copy-done.15, f32[3,6,24,1024,1,1]{3,2,5,4,1,0:T(8,128)S(1)} %copy-done.13), kind=kOutput, calls=%fused_computation.29 | convolution fusion | flops 5453643776 | bytes 3544064 | tf_op jit(solution)/shard_map/dot_general | solution.py:173
  132.0 5.6 %copy.52 = f32[3,6,24,8,2,64]{5,4,3,2,1,0:T(2,128)} copy(f32[3,6,24,8,2,64]{5,2,4,3,1,0:T(8,128)} %pad_maximum_fusion.2) | data formatting | bytes 3538944 | tf_op jit(solution)/shard_map/concatenate | solution.py:69
  137.6 5.5 %reshape.408 = f32[3,6,24,1024]{3,2,1,0:T(8,128)} reshape(f32[3,6,24,8,2,64]{5,4,3,2,1,0:T(2,128)} %copy.52) | data formatting | bytes 3538944 | tf_op jit(solution)/shard_map/reshape | solution.py:69
  143.1 8.2 %maximum_multiply_fusion = f32[3,6,24,8,2,64]{5,4,3,2,1,0:T(2,128)} fusion(f32[3,6,24,8,1,64]{5,4,3,2,1,0:T(1,128)} %get-tuple-element.11, f32[3,6,24,8,1,64]{5,4,3,2,1,0:T(1,128)} %get-tuple-element.10), kind=kLoop, calls=%fused_computation.64 | loop fusion | flops 884736 | bytes 3538944 | tf_op jit(solution)/shard_map/mul | solution.py:203
  151.3 5.6 %mul.744 = f32[3,6,24,1024]{3,2,1,0:T(8,128)} reshape(f32[3,6,24,8,2,64]{5,4,3,2,1,0:T(2,128)} %maximum_multiply_fusion) | data formatting | bytes 3538944 | tf_op jit(solution)/shard_map/mul | solution.py:203
  162.4 4.8 %all-to-all-start.4 = ((f32[4,2,3,6,24,128]{5,1,4,3,2,0:T(2,128)}), f32[4,2,3,6,24,128]{5,1,4,3,2,0:T(2,128)}, u32[]{:S(2)}, u32[]{:S(2)}) async-start(f32[4,2,3,6,24,128]{5,1,4,3,2,0:T(2,128)} %copy.65), calls=%async_computation.4 | async-start | bytes 3538944 | tf_op jit(solution)/shard_map/all_to_all | solution.py:54
  173.2 2.9 copy.59
  176.2 11.6 %all-to-all-done.4 = f32[4,2,3,6,24,128]{5,1,4,3,2,0:T(2,128)} async-done(((f32[4,2,3,6,24,128]{5,1,4,3,2,0:T(2,128)}), f32[4,2,3,6,24,128]{5,1,4,3,2,0:T(2,128)}, u32[]{:S(2)}, u32[]{:S(2)}) %all-to-all-start.4) | async-done | bytes 1769504 | tf_op jit(solution)/shard_map/all_to_all | solution.py:54
  187.7 4.8 %all-to-all-start.3 = ((f32[4,2,3,6,24,128]{5,4,0,3,2,1:T(8,128)}), f32[4,2,3,6,24,128]{5,4,0,3,2,1:T(8,128)}, u32[]{:S(2)}, u32[]{:S(2)}) async-start(f32[4,2,3,6,24,128]{5,4,0,3,2,1:T(8,128)} %copy.59), calls=%async_computation.3 | async-start | bytes 3538944 | tf_op jit(solution)/shard_map/all_to_all | solution.py:54
  194.5 3.7 fusion.353
  198.2 3.8 copy.66
  202.0 9.9 %all-to-all-done.3 = f32[4,2,3,6,24,128]{5,4,0,3,2,1:T(8,128)} async-done(((f32[4,2,3,6,24,128]{5,4,0,3,2,1:T(8,128)}), f32[4,2,3,6,24,128]{5,4,0,3,2,1:T(8,128)}, u32[]{:S(2)}, u32[]{:S(2)}) %all-to-all-start.3) | async-done | bytes 1769504 | tf_op jit(solution)/shard_map/all_to_all | solution.py:54
  212.0 3.7 all-to-all-start.5
  215.7 25.6 %subtract_bitcast_fusion = f32[3,6,3,8,8,128]{5,4,3,2,1,0:T(8,128)S(1)} fusion(f32[3,6,24,1024]{3,2,1,0:T(8,128)} %mul.744, f32[3,6,24,1024]{3,2,1,0:T(8,128)} %reshape.408, s32[1024]{0:T(1024)S(1)} %fusion.220, pred[1024]{0:T(1024)(128)(4,1)S(1)} %copy-done.19, f32[3,6,24,1024]{3,2,1,0:T(8,128)} %fusion.353), kind=kOutput, calls=%fused_computation.164 | convolution fusion | flops 5454528512 | bytes 7083008 | tf_op jit(solution)/shard_map/dot_general | solution.py:173
  243.6 4.8 %all-to-all-start = ((f32[4,2,3,6,24,128]{5,1,4,3,2,0:T(2,128)}), f32[4,2,3,6,24,128]{5,1,4,3,2,0:T(2,128)}, u32[]{:S(2)}, u32[]{:S(2)}) async-start(f32[4,2,3,6,24,128]{5,1,4,3,2,0:T(2,128)} %copy.54), calls=%async_computation | async-start | bytes 3538944 | tf_op jit(solution)/shard_map/all_to_all | solution.py:54
  250.3 3.7 convolution_bitcast_fusion.4
  254.0 3.7 convolution_bitcast_fusion.5
  260.2 3.7 convolution_bitcast_fusion.3
  263.8 3.1 all-to-all-done
  266.9 3.8 copy.55
  270.8 4.9 %all-to-all-start.1 = ((f32[4,2,3,6,24,128]{5,0,4,3,2,1:T(4,128)}), f32[4,2,3,6,24,128]{5,0,4,3,2,1:T(4,128)}, u32[]{:S(2)}, u32[]{:S(2)}) async-start(f32[4,2,3,6,24,128]{5,0,4,3,2,1:T(4,128)} %copy.55), calls=%async_computation.1 | async-start | bytes 3538944 | tf_op jit(solution)/shard_map/all_to_all | solution.py:54
  275.6 4.1 slice_add_fusion.1
  281.4 2.9 copy.62
  287.8 2.9 copy.63
  290.8 3.1 slice_add_fusion
  299.8 2.9 copy.70
  313.9 4.0 collective-permute-start.3
  320.5 11.4 %collective-permute-done.2 = f32[4,3,192,128]{3,2,1,0:T(8,128)} collective-permute-done((f32[4,3,192,128]{3,2,1,0:T(8,128)}, f32[4,3,192,128]{3,2,1,0:T(8,128)}, u32[]{:S(2)}, u32[]{:S(2)}) %collective-permute-start.2) | collective-permute-done | bytes 1179680 | tf_op jit(solution)/shard_map/ppermute | solution.py:29
  332.0 2.9 copy.71
  334.9 2.9 copy.73
  337.8 3.6 multiply_subtract_fusion.1
  342.7 2.9 copy.72
  345.6 2.7 pad_maximum_fusion.11
  348.2 2.9 copy.74
  363.7 2.7 copy.76
  374.3 3.2 fusion.142
  402.1 5.7 %all-to-all-start.6 = ((f32[3,6,192,128]{3,1,0,2:T(8,128)}), f32[3,6,192,128]{3,1,0,2:T(8,128)}, u32[]{:S(2)}, u32[]{:S(2)}) async-start(f32[3,6,192,128]{3,1,0,2:T(8,128)} %copy.82), calls=%async_computation.6 | async-start | bytes 4718592 | tf_op jit(solution)/shard_map/all_to_all | solution.py:266
  407.8 19.5 %fusion.351 = f32[1024,1024,1,1]{1,0,3,2:T(8,128)} fusion(f32[1024]{0:T(1024)S(1)} %compare_select_fusion.2, s32[1024]{0:T(1024)S(1)} %fusion.220, pred[1024]{0:T(1024)(128)(4,1)S(1)} %copy-done.20), kind=kLoop, calls=%fused_computation.26.clone.clone.clone.1 | loop fusion | flops 18874368 | bytes 4203520 | tf_op jit(solution)/shard_map/dot_general | solution.py:268
  427.3 13.3 %all-to-all-done.6 = f32[3,6,192,128]{3,1,0,2:T(8,128)} async-done(((f32[3,6,192,128]{3,1,0,2:T(8,128)}), f32[3,6,192,128]{3,1,0,2:T(8,128)}, u32[]{:S(2)}, u32[]{:S(2)}) %all-to-all-start.6) | async-done | bytes 1769504 | tf_op jit(solution)/shard_map/all_to_all | solution.py:266
  440.6 3.9 copy.99
  446.0 8.5 %multiply_add_fusion = f32[3,6,24,1024]{3,2,1,0:T(8,128)} fusion(f32[3,6,24,1024]{3,2,1,0:T(8,128)S(1)} %copy-done, f32[3,6,24,1024]{3,2,1,0:T(8,128)S(1)} %dot_general.56, f32[1024,1024,1,1]{1,0,3,2:T(8,128)} %fusion.351), kind=kOutput, calls=%fused_computation.162 | convolution fusion | flops 5436702720 | bytes 9502720 | tf_op jit(solution)/shard_map/dot_general | solution.py:268
  (132 shorter events, 101.4 us)
Async XLA Ops:
  0.6 6.9 %copy-start = (f32[3,6,24,1024]{3,2,1,0:T(8,128)S(1)}, f32[3,6,24,1024]{3,2,1,0:T(8,128)}, u32[]{:S(2)}) copy-start(f32[3,6,24,1024]{3,2,1,0:T(8,128)} %param.6) | copy-start | bytes 5308420
  3.6 157.8 %collective-permute-start = (f32[3,3,24,1024]{3,2,1,0:T(8,128)}, f32[3,3,24,1024]{3,2,1,0:T(8,128)S(1)}, u32[]{:S(2)}, u32[]{:S(2)}) collective-permute-start(f32[3,3,24,1024]{3,2,1,0:T(8,128)} %get-tuple-element.33), channel_id=1, source_target_pairs={{0,8},{8,16},{16,24},{24,32},{32,40},{40,48},{48,56},{56,64},{64,7... | collective-permute-start | bytes 2654216 | tf_op jit(solution)/shard_map/ppermute | solution.py:29
  3.6 164.6 %collective-permute-start.1 = (f32[3,3,24,1024]{3,2,1,0:T(8,128)}, f32[3,3,24,1024]{3,2,1,0:T(8,128)S(1)}, u32[]{:S(2)}, u32[]{:S(2)}) collective-permute-start(f32[3,3,24,1024]{3,2,1,0:T(8,128)} %get-tuple-element.32), channel_id=1, source_target_pairs={{8,0},{16,8},{24,16},{32,24},{40,32},{48,40},{56,48},{64,56},{72,6... | collective-permute-start | bytes 2654216 | tf_op jit(solution)/shard_map/ppermute | solution.py:31
  40.3 122.1 %all-to-all-start.2 = ((f32[4,2,3,6,24,128]{5,4,1,3,2,0:T(8,128)}), f32[4,2,3,6,24,128]{5,4,1,3,2,0:T(8,128)}, u32[]{:S(2)}, u32[]{:S(2)}) async-start(f32[4,2,3,6,24,128]{5,4,1,3,2,0:T(8,128)} %copy.58), calls=%async_computation.2 | async-start | bytes 3538944 | tf_op jit(solution)/shard_map/all_to_all | solution.py:54
  46.7 2.6 copy-start.18
  77.8 8.8 %copy-start.13 = (f32[3,6,24,1024,1,1]{3,2,5,4,1,0:T(8,128)S(1)}, f32[3,6,24,1024,1,1]{3,2,5,4,1,0:T(8,128)}, u32[]{:S(2)}) copy-start(f32[3,6,24,1024,1,1]{3,2,5,4,1,0:T(8,128)} %fusion.349) | copy-start | bytes 5308420
  77.8 8.8 %copy-start.15 = (pred[8,2,64]{2,1,0:T(4,128)(4,1)S(1)}, pred[8,2,64]{2,1,0:T(4,128)(4,1)}, u32[]{:S(2)}) copy-start(pred[8,2,64]{2,1,0:T(4,128)(4,1)} %fusion.213) | copy-start | bytes 3076
  162.4 25.3 %all-to-all-start.4 = ((f32[4,2,3,6,24,128]{5,1,4,3,2,0:T(2,128)}), f32[4,2,3,6,24,128]{5,1,4,3,2,0:T(2,128)}, u32[]{:S(2)}, u32[]{:S(2)}) async-start(f32[4,2,3,6,24,128]{5,1,4,3,2,0:T(2,128)} %copy.65), calls=%async_computation.4 | async-start | bytes 3538944 | tf_op jit(solution)/shard_map/all_to_all | solution.py:54
  168.2 1.8 copy-start.8
  168.2 0.9 copy-start.3
  170.0 1.2 copy-start.4
  187.7 24.2 %all-to-all-start.3 = ((f32[4,2,3,6,24,128]{5,4,0,3,2,1:T(8,128)}), f32[4,2,3,6,24,128]{5,4,0,3,2,1:T(8,128)}, u32[]{:S(2)}, u32[]{:S(2)}) async-start(f32[4,2,3,6,24,128]{5,4,0,3,2,1:T(8,128)} %copy.59), calls=%async_computation.3 | async-start | bytes 3538944 | tf_op jit(solution)/shard_map/all_to_all | solution.py:54
  192.5 1.9 copy-start.11
  192.5 1.9 copy-start.12
  202.0 13.7 %copy-start.19 = (pred[1024]{0:T(1024)(128)(4,1)S(1)}, pred[1024]{0:T(1024)(128)(4,1)}, u32[]{:S(2)}) copy-start(pred[1024]{0:T(1024)(128)(4,1)} %copy-done.18) | copy-start | bytes 3076
  212.0 31.6 %all-to-all-start.5 = ((f32[4,2,3,6,24,128]{5,0,4,3,2,1:T(4,128)}), f32[4,2,3,6,24,128]{5,0,4,3,2,1:T(4,128)S(1)}, u32[]{:S(2)}, u32[]{:S(2)}) async-start(f32[4,2,3,6,24,128]{5,0,4,3,2,1:T(4,128)} %copy.66), calls=%async_computation.5 | async-start | bytes 3538944 | tf_op jit(solution)/shard_map/all_to_all | solution.py:54
  243.6 23.3 %all-to-all-start = ((f32[4,2,3,6,24,128]{5,1,4,3,2,0:T(2,128)}), f32[4,2,3,6,24,128]{5,1,4,3,2,0:T(2,128)}, u32[]{:S(2)}, u32[]{:S(2)}) async-start(f32[4,2,3,6,24,128]{5,1,4,3,2,0:T(2,128)} %copy.54), calls=%async_computation | async-start | bytes 3538944 | tf_op jit(solution)/shard_map/all_to_all | solution.py:54
  270.8 32.0 %all-to-all-start.1 = ((f32[4,2,3,6,24,128]{5,0,4,3,2,1:T(4,128)}), f32[4,2,3,6,24,128]{5,0,4,3,2,1:T(4,128)}, u32[]{:S(2)}, u32[]{:S(2)}) async-start(f32[4,2,3,6,24,128]{5,0,4,3,2,1:T(4,128)} %copy.55), calls=%async_computation.1 | async-start | bytes 3538944 | tf_op jit(solution)/shard_map/all_to_all | solution.py:54
  309.3 1.5 copy-start.5
  309.3 2.0 copy-start.6
  311.3 1.1 copy-start.9
  313.9 18.1 %collective-permute-start.2 = (f32[4,3,192,128]{3,2,1,0:T(8,128)}, f32[4,3,192,128]{3,2,1,0:T(8,128)}, u32[]{:S(2)}, u32[]{:S(2)}) collective-permute-start(f32[4,3,192,128]{3,2,1,0:T(8,128)} %get-tuple-element.24), channel_id=1, source_target_pairs={{0,8},{8,16},{16,24},{24,32},{32,40},{40,48},{48,56},{56,64},{64,7... | collective-permute-start | bytes 3538952 | tf_op jit(solution)/shard_map/ppermute | solution.py:29
  313.9 20.9 %collective-permute-start.3 = (f32[4,3,192,128]{3,2,1,0:T(8,128)}, f32[4,3,192,128]{3,2,1,0:T(8,128)}, u32[]{:S(2)}, u32[]{:S(2)}) collective-permute-start(f32[4,3,192,128]{3,2,1,0:T(8,128)} %get-tuple-element.25), channel_id=1, source_target_pairs={{8,0},{16,8},{24,16},{32,24},{40,32},{48,40},{56,48},{64,56},{72,6... | collective-permute-start | bytes 3538952 | tf_op jit(solution)/shard_map/ppermute | solution.py:31
  334.9 2.9 copy-start.17
  351.1 1.6 copy-start.7
  352.8 1.5 copy-start.10
  354.8 2.2 copy-start.1
  358.4 2.7 copy-start.16
  374.3 3.2 copy-start.14
  392.8 2.5 copy-start.2
  402.1 5.7 %copy-start.20 = (pred[1024]{0:T(1024)(128)(4,1)S(1)}, pred[1024]{0:T(1024)(128)(4,1)}, u32[]{:S(2)}) copy-start(pred[1024]{0:T(1024)(128)(4,1)} %copy-done.18) | copy-start | bytes 3076
  402.1 38.5 %all-to-all-start.6 = ((f32[3,6,192,128]{3,1,0,2:T(8,128)}), f32[3,6,192,128]{3,1,0,2:T(8,128)}, u32[]{:S(2)}, u32[]{:S(2)}) async-start(f32[3,6,192,128]{3,1,0,2:T(8,128)} %copy.82), calls=%async_computation.6 | async-start | bytes 4718592 | tf_op jit(solution)/shard_map/all_to_all | solution.py:266
where the time goes:
time: 462 us; the launch traced here: 455 us
  matrix products  153 us (33%)
  local copies, waits for them, and re-layouts  105 us (23%)
  other arithmetic  103 us (22%)
  waiting for transfers between devices  49.3 us (11%)
  starting transfers between devices  42.2 us (9%)
    dot_general x4, matrix products, to_modes(): jnp.dot(flat, forward_y, precision=highest, preferred_element_type=jnp.fl...  121 us
    all_to_all x6, starting transfers between devices, exchange_in_order(): out = lax.all_to_all(out, axes[k], k, k, tiled=True)  28.6 us
    all_to_all x6, waiting for transfers between devices, exchange_in_order(): out = lax.all_to_all(out, axes[k], k, k, tiled=True)  24.6 us
    reshape x6, local copies, waits for them, and re-layouts, join_parts(): return jnp.concatenate([real_part, imag_part], axis=-2).reshape(shape)  19.5 us
    dot_general x1, other arithmetic, local(): jnp.dot(flat, inverse_y, precision=highest, preferred_element_type=jnp.fl...  19.5 us
    all_to_all x1, waiting for transfers between devices, local(): piece = lax.all_to_all(spatial, YZ, split_axis=2, concat_axis=3, tiled=True)  13.3 us
    concatenate x8, other arithmetic, join_parts(): return jnp.concatenate([real_part, imag_part], axis=-2).reshape(shape)  12.9 us
    dot_general x4, matrix products, z_apply(): with_cos = jnp.einsum('wz,nxzk->nxwk', cos_z, packed, precision=highest)  12.3 us
  transfers between devices with their start and end apart: 11, of which 5 were waited for; matrix products, arithmetic and copies ran while one was open for 57% of the time, Pallas kernels for 0%

commit v1 on v0

v1 whole, which is shorter than its diff:
```python
import functools
import math

import jax
import jax.numpy as jnp
import numpy as np
from jax import lax
from jax.experimental import pallas as pl
from jax.experimental.pallas import tpu as pltpu
from jax.sharding import PartitionSpec as P

viscosity = 0.05
time_step = 0.2
keep_weight = -5.0 / 9.0
section_weight = 15.0 / 16.0
shear_param = 1.5
fraction = 0.375
GROUPS = 8
MESH = pl.DeviceIdType.MESH
F32 = jnp.float32
BF16 = jnp.bfloat16


def tables(width_y, depth_z):
    half = width_y // (2 * GROUPS)
    lanes = np.arange(width_y)
    mode = lanes // (2 * half) * half + lanes % half
    is_im = (lanes // half) % 2 == 1
    coarse = np.arange(width_y // half)
    fine = np.arange(half)

    def angle(n, k):
        return 2.0 * np.pi / width_y * ((n[:, None] * k[None, :]) % width_y)

    scale = 1.0 / math.sqrt(width_y)
    alpha = angle(coarse * half, mode)
    beta = angle(fine, mode)
    fwd_coarse = np.concatenate([np.cos(alpha), np.sin(alpha)])
    fwd_fine = scale * np.stack(
        [
            np.where(is_im[None], -np.sin(beta), np.cos(beta)),
            np.where(is_im[None], -np.cos(beta), -np.sin(beta)),
        ]
    )
    cells = np.arange(width_y)
    alpha = angle(np.arange(GROUPS) * half, cells)
    beta = angle(fine, cells)
    inv_coarse = np.concatenate([np.cos(alpha), np.sin(alpha)])
    inv_fine = (2.0 * section_weight * scale) * np.stack(
        [
            np.concatenate([np.cos(beta), -np.sin(beta)]),
            np.concatenate([-np.sin(beta), -np.cos(beta)]),
        ]
    )
    wave_y = 2.0 * np.pi / width_y * mode[None, :]
    m = np.arange(depth_z)
    signed = np.where(m < depth_z // 2, m, m - depth_z)
    wave_z = (2.0 * np.pi / depth_z * signed)[:, None]
    angle_z = 2.0 * np.pi / depth_z * ((m[:, None] * m[None, :]) % depth_z)
    forward = np.exp(-1j * angle_z) / math.sqrt(depth_z)
    mats = [
        forward,
        1j * wave_z * forward,
        -viscosity * wave_z * wave_z * forward,
        np.exp(1j * angle_z) / math.sqrt(depth_z),
    ]
    stacked = []
    for mat in mats:
        both = np.concatenate([mat.real, mat.imag]).astype(np.float32)
        high = both.astype(BF16)
        low = (both - high.astype(np.float32)).astype(BF16)
        stacked.append(np.concatenate([high, low]))
    as32 = lambda v: jnp.asarray(np.asarray(v, np.float32))
    return (
        as32(fwd_coarse),
        as32(fwd_fine),
        as32(inv_coarse),
        as32(inv_fine),
        as32(wave_y),
        as32(np.broadcast_to(wave_z, (depth_z, 2 * half))),
        jnp.asarray(np.stack(stacked)),
    )


def split(value):
    high = value.astype(BF16)
    low = (value - high.astype(F32)).astype(BF16)
    return high, low


def mm(a, b):
    return jnp.dot(a, b, preferred_element_type=F32)


def body(
    slabs,
    shift_ref,
    vel_hbm,
    qold_hbm,
    guess_hbm,
    edge_hbm,
    fcoarse_hbm,
    ffine_hbm,
    icoarse_hbm,
    ifine_hbm,
    wavey_hbm,
    wavez_hbm,
    zmat_hbm,
    vnext_hbm,
    qnext_hbm,
    pout_hbm,
    ghost,
    fcoarse,
    ffine,
    icoarse,
    ifine,
    wavey,
    wavez,
    zmat,
    edge,
    qold,
    f_hi,
    f_lo,
    l_hi,
    l_lo,
    spec_u,
    spec_c,
    spec_w,
    got_u,
    got_c,
    got_w,
    tend,
    tend_x,
    cross,
    guess,
    recip,
    press,
    spatial,
    got_s,
    load_sem,
    halo_send,
    halo_recv,
    fwd_send,
    fwd_recv,
    inv_send,
    inv_recv,
    out_sem,
):
    gx = lax.axis_index("gx")
    me = lax.axis_index("yz")
    my_z = me // 2
    right = lax.rem(gx + 1, slabs)
    left = lax.rem(gx + slabs - 1, slabs)
    planes = 6
    rows = 24
    width = 1024
    depth = 192
    lanes = 128
    half = 64
    flat = planes * rows * 3

    def peer(d):
        return lax.rem(me + d, GROUPS)

    loads = [
        (vel_hbm, ghost.at[:, pl.ds(3, planes)]),
        (fcoarse_hbm, fcoarse),
        (ffine_hbm, ffine),
        (guess_hbm, guess.at[pl.ds(3, planes)]),
        (wavey_hbm, wavey),
        (edge_hbm, edge),
        (zmat_hbm, zmat),
        (wavez_hbm, wavez),
        (icoarse_hbm, icoarse),
        (ifine_hbm, ifine),
        (qold_hbm, qold),
    ]
    loads = [pltpu.make_async_copy(s, d, load_sem.at[i]) for i, (s, d) in enumerate(loads)]
    for copy in loads:
        copy.start()

    barrier = pltpu.get_barrier_semaphore()
    for d in range(1, GROUPS):
        pl.semaphore_signal(
            barrier, inc=1, device_id={"gx": gx, "yz": peer(d)}, device_id_type=MESH
        )
    for side in (left, right):
        pl.semaphore_signal(barrier, inc=1, device_id={"gx": side, "yz": me}, device_id_type=MESH)

    def halo(ref, count, own, slot, lead):
        def at(start):
            return ref.at[:, pl.ds(start, count)] if lead else ref.at[pl.ds(start, count)]

        to_left = pltpu.make_async_remote_copy(
            src_ref=at(count), dst_ref=at(count + own), send_sem=halo_send.at[slot],
            recv_sem=halo_recv.at[slot], device_id={"gx": left, "yz": me}, device_id_type=MESH,
        )
        to_right = pltpu.make_async_remote_copy(
            src_ref=at(own), dst_ref=at(0), send_sem=halo_send.at[slot + 1],
            recv_sem=halo_recv.at[slot + 1], device_id={"gx": right, "yz": me}, device_id_type=MESH,
        )
        return to_left, to_right

    loads[0].wait()
    loads[3].wait()
    pl.semaphore_wait(barrier, GROUPS + 1)
    vel_halo = halo(ghost, 3, planes, 0, True)
    guess_halo = halo(guess, 3, planes, 2, False)
    for copy in vel_halo + guess_halo:
        copy.start()

    def store_split(at, value):
        high, low = split(value)
        where = pl.ds(pl.multiple_of(at, 48), 48)
        l_hi[where, :] = high
        l_lo[where, :] = low

    def build(dst_hi, dst_lo, coarse, fine, steps, length):
        def step(a, carry):
            value = (
                coarse[pl.ds(a, 1), :] * fine[0] + coarse[pl.ds(a + steps, 1), :] * fine[1]
            )
            high, low = split(value)
            where = pl.ds(pl.multiple_of(a * length, length), length)
            dst_hi[where, :] = high
            dst_lo[where, :] = low
            return carry

        lax.fori_loop(0, steps, step, 0)

    def pairs_loop(write):
        def step(i, carry):
            write(i // 3, lax.rem(i, 3) * 2, i * 48)
            return carry

        lax.fori_loop(0, 9, step, 0)

    def put_u(c, p, at):
        store_split(at, ghost[c, pl.ds(3 + p, 2)].reshape(48, width))

    loads[1].wait()
    loads[2].wait()
    build(f_hi, f_lo, fcoarse, ffine, width // half, half)
    pairs_loop(put_u)

    def to_modes(at, col):
        a_hi = l_hi[pl.ds(at, flat), :]
        a_lo = l_lo[pl.ds(at, flat), :]
        b_hi = f_hi[:, pl.ds(col, 256)]
        b_lo = f_lo[:, pl.ds(col, 256)]
        return mm(a_hi, b_hi) + mm(a_lo, b_hi) + mm(a_hi, b_lo)

    def fwd_copy(spec, got, kind, dest, first, count):
        return pltpu.make_async_remote_copy(
            src_ref=spec.at[pl.ds(first, count), :, pl.ds(pl.multiple_of(dest * lanes, lanes), lanes)],
            dst_ref=got.at[pl.ds(first, count), pl.ds(pl.multiple_of(me * rows, 8), rows), :],
            send_sem=fwd_send.at[kind, dest],
            recv_sem=fwd_recv.at[kind, me],
            device_id={"gx": gx, "yz": dest},
            device_id_type=MESH,
        )

    def fwd_own(spec, got, kind, first, count):
        return pltpu.make_async_copy(
            spec.at[pl.ds(first, count), :, pl.ds(pl.multiple_of(me * lanes, lanes), lanes)],
            got.at[pl.ds(first, count), pl.ds(pl.multiple_of(me * rows, 8), rows), :],
            fwd_recv.at[kind, me],
        )

    def fwd_wait(got, kind, first, count):
        def step(d, carry):
            src = peer(d)
            pltpu.make_async_remote_copy(
                src_ref=got.at[pl.ds(first, count), pl.ds(pl.multiple_of(src * rows, 8), rows), :],
                dst_ref=got.at[pl.ds(first, count), pl.ds(pl.multiple_of(src * rows, 8), rows), :],
                send_sem=fwd_send.at[kind, src],
                recv_sem=fwd_recv.at[kind, src],
                device_id={"gx": gx, "yz": src},
                device_id_type=MESH,
            ).wait_recv()
            return carry

        lax.fori_loop(1, GROUPS, step, 0)

    partner = me + 1 - 2 * lax.rem(me, 2)

    def transform_and_send(spec, got, kind):
        def step(i, carry):
            target = lax.rem(my_z + 1 + i, 4)
            col = pl.multiple_of(target * 256, 256)
            spec[:, :, pl.ds(col, 256)] = to_modes(0, col).reshape(18, rows, 256)
            for side in range(2):
                dest = target * 2 + side

                @pl.when(dest != me)
                def _():
                    fwd_copy(spec, got, kind, dest, 0, 18).start()

            return carry

        lax.fori_loop(0, 4, step, 0)
        fwd_own(spec, got, kind, 0, 18).start()

    transform_and_send(spec_u, got_u, 0)

    def put_c(c, p, at):
        u_z = ghost[2, pl.ds(3 + p, 2)]
        store_split(at, (-u_z * ghost[c, pl.ds(3 + p, 2)]).reshape(48, width))

    pairs_loop(put_c)
    transform_and_send(spec_c, got_c, 1)

    for copy in vel_halo:
        copy.wait_recv()
    shift = shift_ref[0]

    def moved(value, amount, extra):
        once = pltpu.roll(value, amount, 1)
        return (1.0 - fraction) * once + fraction * pltpu.roll(once, extra, 1)

    def fix(start, amount, extra):
        def step(i, carry):
            c, p = i // 3, lax.rem(i, 3) + start
            ghost[c, p] = moved(ghost[c, p], amount, extra)
            return carry

        lax.fori_loop(0, 9, step, 0)

    @pl.when(gx == 0)
    def _():
        fix(0, lax.rem(width - shift, width), width - 1)

    @pl.when(gx == slabs - 1)
    def _():
        fix(planes + 3, shift, 1)

    total_x = planes * slabs
    omega = 2.0 / total_x

    def put_ab(i, carry):
        c, p = i // 3, lax.rem(i, 3) * 2
        terms_a = []
        terms_b = []
        for q in range(2):
            at = p + q + 3
            u_x = [ghost[0, at + o] for o in range(-3, 4)]
            u_i = [ghost[c, at + o] for o in range(-3, 4)]
            prod = [x * y for x, y in zip(u_x, u_i)]
            first = (
                (45.0 / 60.0) * (prod[4] - prod[2])
                - (9.0 / 60.0) * (prod[5] - prod[1])
                + (1.0 / 60.0) * (prod[6] - prod[0])
            )
            second = (
                (2.0 / 180.0) * (u_i[6] + u_i[0])
                - (27.0 / 180.0) * (u_i[5] + u_i[1])
                + (270.0 / 180.0) * (u_i[4] + u_i[2])
                - (490.0 / 180.0) * u_i[3]
            )
            u_y = ghost[1, at]
            weight_y = jnp.where(c == 0, 2.0 * omega, 0.0).astype(F32)
            weight_x = jnp.where(c == 1, -(2.0 - shear_param) * omega, 0.0).astype(F32)
            terms_a.append(viscosity * second - first + (weight_y * u_y + weight_x * u_x[3]))
            place = (gx * planes + p + q).astype(F32) + 0.5 - total_x / 2.0
            background = -shear_param * omega * place
            terms_b.append(-(u_y + background) * u_i[3])
        store_split(i * 48, jnp.concatenate(terms_a, axis=0))
        store_split(flat + i * 48, jnp.concatenate(terms_b, axis=0))
        return carry

    lax.fori_loop(0, 9, put_ab, 0)

    loads[4].wait()
    sign = jnp.where(lax.broadcasted_iota(jnp.int32, (1, lanes), 1) < half, -1.0, 1.0).astype(F32)

    def turned(value):
        return pltpu.roll(value, half, 1) * sign

    def combine(i, carry):
        target = lax.rem(my_z + 1 + i, 4)
        col = pl.multiple_of(target * 256, 256)
        ya = to_modes(0, col)
        yb = to_modes(flat, col)
        for side in range(2):
            wide = pl.ds(pl.multiple_of(col + side * lanes, lanes), lanes)
            cut = slice(side * lanes, (side + 1) * lanes)
            ky = wavey[0:1, wide]
            yu = spec_u[:, :, wide].reshape(flat, lanes)
            out = ya[:, cut] + turned(yb[:, cut]) * ky - (viscosity * ky * ky) * yu
            spec_w[:, :, wide] = out.reshape(18, rows, lanes)
        return carry

    lax.fori_loop(0, 4, combine, 0)
    for c in range(3):
        def send(i, carry, c=c):
            target = lax.rem(my_z + 1 + i, 4)
            for side in range(2):
                dest = target * 2 + side

                @pl.when(dest != me)
                def _():
                    fwd_copy(spec_w, got_w, 2 + c, dest, c * planes, planes).start()

            return carry

        lax.fori_loop(0, 4, send, 0)
        fwd_own(spec_w, got_w, 2 + c, c * planes, planes).start()

    loads[5].wait()
    loads[6].wait()
    loads[7].wait()
    own_ky = wavey[0:1, pl.ds(pl.multiple_of(me * lanes, lanes), lanes)]
    recip[...] = 1.0 / (2.0 + own_ky * own_ky + wavez[...] * wavez[...])

    def rotate_ends(ref, count, own):
        cosine = edge[0:1, :]
        sine = edge[1:2, :]

        @pl.when(gx == 0)
        def _():
            for j in range(count):
                value = ref[j]
                ref[j] = value * cosine + turned(value) * sine

        @pl.when(gx == slabs - 1)
        def _():
            for j in range(own + count, own + 2 * count):
                value = ref[j]
                ref[j] = value * cosine - turned(value) * sine

    for copy in guess_halo:
        copy.wait_recv()
    rotate_ends(guess, 3, planes)

    def z_pair(ref, at, kind):
        value = jnp.concatenate([ref[at], ref[at + 1]], axis=1)
        high, low = split(value)
        mat = zmat[kind]
        return mm(mat, high), mm(zmat[kind, pl.ds(0, 2 * depth)], low)

    def z_join(parts):
        total = sum(wide[: 2 * depth] + wide[2 * depth :] + low for wide, low in parts)
        out = []
        for q in range(2):
            cut = slice(q * lanes, (q + 1) * lanes)
            out.append(total[:depth, cut] + turned(total[depth:, cut]))
        return out

    for copy in (fwd_own(spec_u, got_u, 0, 0, 18), fwd_own(spec_c, got_c, 1, 0, 18)):
        copy.wait()
    fwd_wait(got_u, 0, 0, 18)
    fwd_wait(got_c, 1, 0, 18)

    def z_first(i, carry):
        at = i * 2
        first, second = z_join([z_pair(got_c, at, 1), z_pair(got_u, at, 2)])
        tend[at] = first
        tend[at + 1] = second
        return carry

    lax.fori_loop(0, 9, z_first, 0)

    loads[8].wait()
    loads[9].wait()
    build(f_hi, f_lo, icoarse, ifine, GROUPS, 2 * half)
    head_hi = f_hi[0:16, :]
    head_lo = f_lo[0:16, :]
    top = lax.broadcasted_iota(jnp.int32, (16, width), 0) == 0
    f_hi[0:16, :] = jnp.where(top, head_hi.astype(F32) * 0.5, head_hi.astype(F32)).astype(BF16)
    f_lo[0:16, :] = jnp.where(top, head_lo.astype(F32) * 0.5, head_lo.astype(F32)).astype(BF16)

    def z_last(c, write):
        fwd_own(spec_w, got_w, 2 + c, c * planes, planes).wait()
        fwd_wait(got_w, 2 + c, c * planes, planes)

        def step(i, carry):
            at = c * planes + i * 2
            values = z_join([z_pair(got_w, at, 0)])
            for q in range(2):
                write(i * 2 + q, at + q, tend[at + q] + values[q])
            return carry

        lax.fori_loop(0, 3, step, 0)

    def write_x(p, at, value):
        tend[at] = value
        tend_x[p + 3] = value

    z_last(0, write_x)
    x_halo = halo(tend_x, 3, planes, 4, False)
    for copy in x_halo:
        copy.start()

    def write_y(p, at, value):
        tend[at] = value
        cross[p + 2] = turned(value) * own_ky

    z_last(1, write_y)

    def write_z(p, at, value):
        tend[at] = value
        cross[p + 2] = cross[p + 2] + turned(value) * wavez[...]

    z_last(2, write_z)
    cross_halo = halo(cross, 2, planes, 6, False)
    for copy in cross_halo:
        copy.start()
    loads[10].wait()
    for copy in x_halo:
        copy.wait_recv()
    rotate_ends(tend_x, 3, planes)
    for copy in cross_halo:
        copy.wait_recv()
    rotate_ends(cross, 2, planes)

    def diverge(j, carry):
        got_u[j] = 0.5 * (tend_x[j + 2] - tend_x[j]) + cross[j]
        return carry

    lax.fori_loop(0, planes + 4, diverge, 0)

    def sweep_a(j, carry):
        got_c[j] = (guess[j + 2] + guess[j] - got_u[j]) * recip[...]
        return carry

    lax.fori_loop(0, planes + 4, sweep_a, 0)

    def sweep_b(j, carry):
        press[j] = (got_c[j + 2] + got_c[j] - got_u[j + 1]) * recip[...]
        return carry

    lax.fori_loop(0, planes + 2, sweep_b, 0)
    pltpu.make_async_copy(press.at[pl.ds(1, planes)], pout_hbm, out_sem.at[0]).start()

    def inv_copy(c, dest):
        return pltpu.make_async_remote_copy(
            src_ref=spatial.at[pl.ds(c * planes, planes), pl.ds(pl.multiple_of(dest * rows, 8), rows), :],
            dst_ref=got_s.at[pl.ds(c * planes, planes), :, pl.ds(pl.multiple_of(me * lanes, lanes), lanes)],
            send_sem=inv_send.at[c, dest],
            recv_sem=inv_recv.at[c, me],
            device_id={"gx": gx, "yz": dest},
            device_id_type=MESH,
        )

    def inv_own(c):
        return pltpu.make_async_copy(
            spatial.at[pl.ds(c * planes, planes), pl.ds(pl.multiple_of(me * rows, 8), rows), :],
            got_s.at[pl.ds(c * planes, planes), :, pl.ds(pl.multiple_of(me * lanes, lanes), lanes)],
            inv_recv.at[c, me],
        )

    for c in range(3):
        def update(p, carry, c=c):
            at = c * planes + p
            here = press[p + 1]
            if c == 0:
                slope = 0.5 * (press[p + 2] - press[p])
            elif c == 1:
                slope = turned(here) * own_ky
            else:
                slope = turned(here) * wavez[...]
            qold[c, p] = keep_weight * qold[c, p] + time_step * (tend[at] - slope)
            return carry

        lax.fori_loop(0, planes, update, 0)

        def back(i, carry, c=c):
            at = c * planes + i * 2
            values = z_join([z_pair(qold.at[c], i * 2, 3)])
            spatial[at] = values[0]
            spatial[at + 1] = values[1]
            return carry

        lax.fori_loop(0, 3, back, 0)

        def send(i, carry, c=c):
            inv_copy(c, peer(i)).start()
            return carry

        lax.fori_loop(1, GROUPS, send, 0)
        inv_own(c).start()
    pltpu.make_async_copy(qold, qnext_hbm, out_sem.at[1]).start()

    rows_c = planes * rows
    for c in range(3):
        inv_own(c).wait()

        def arrive(d, carry, c=c):
            src = peer(d)
            where = got_s.at[pl.ds(c * planes, planes), :, pl.ds(pl.multiple_of(src * lanes, lanes), lanes)]
            pltpu.make_async_remote_copy(
                src_ref=where, dst_ref=where, send_sem=inv_send.at[c, src],
                recv_sem=inv_recv.at[c, src], device_id={"gx": gx, "yz": src}, device_id_type=MESH,
            ).wait_recv()
            return carry

        lax.fori_loop(1, GROUPS, arrive, 0)
        high, low = split(got_s[pl.ds(c * planes, planes)].reshape(rows_c, width))
        l_hi[pl.ds(c * rows_c, rows_c), :] = high
        l_lo[pl.ds(c * rows_c, rows_c), :] = low

        def step(i, carry, c=c):
            cols = pl.ds(pl.multiple_of(i * 256, 256), 256)
            a_hi = l_hi[pl.ds(c * rows_c, rows_c), :]
            a_lo = l_lo[pl.ds(c * rows_c, rows_c), :]
            out = mm(a_hi, f_hi[:, cols]) + mm(a_lo, f_hi[:, cols]) + mm(a_hi, f_lo[:, cols])
            spec_u[pl.ds(c * planes, planes), :, cols] = (
                ghost[c, pl.ds(3, planes), :, cols] + out.reshape(planes, rows, 256)
            )
            return carry

        if c == 0:
            def sent(d, carry):
                fwd_copy(spec_u, got_u, 0, peer(d), 0, 18).wait_send()
                return carry

            lax.fori_loop(1, GROUPS, sent, 0)
        lax.fori_loop(0, 4, step, 0)
        pltpu.make_async_copy(
            spec_u.at[pl.ds(c * planes, planes)], vnext_hbm.at[c], out_sem.at[2 + c]
        ).start()

    def drain(d, carry):
        dest = peer(d)
        fwd_copy(spec_c, got_c, 1, dest, 0, 18).wait_send()
        for c in range(3):
            fwd_copy(spec_w, got_w, 2 + c, dest, c * planes, planes).wait_send()
            inv_copy(c, dest).wait_send()
        return carry

    lax.fori_loop(1, GROUPS, drain, 0)
    for copy in vel_halo + guess_halo + x_halo + cross_halo:
        copy.wait_send()
    pltpu.make_async_copy(press.at[pl.ds(1, planes)], pout_hbm, out_sem.at[0]).wait()
    pltpu.make_async_copy(qold, qnext_hbm, out_sem.at[1]).wait()
    for c in range(3):
        pltpu.make_async_copy(
            spec_u.at[pl.ds(c * planes, planes)], vnext_hbm.at[c], out_sem.at[2 + c]
        ).wait()


def local(slabs, vel, q_old, pressure_guess, shear_shift):
    width = vel.shape[3]
    depth = q_old.shape[2]
    half = width // (2 * GROUPS)
    planes, rows = vel.shape[1], vel.shape[2]
    consts = tables(width, depth)
    modes = lax.axis_index("yz") * half + jnp.arange(2 * half, dtype=jnp.int32) % half
    angle = (2.0 * math.pi / width) * (
        (modes * shear_shift[0] % width).astype(F32) + fraction * modes.astype(F32)
    )
    edge = jnp.stack([jnp.cos(angle), jnp.sin(angle)])
    any_spec = pl.BlockSpec(memory_space=pl.ANY)
    vmem = lambda *shape: pltpu.VMEM(shape, F32)
    wide = lambda n: pltpu.VMEM((n, depth, 2 * half), F32)
    flat = 3 * planes * rows
    scratch = [
        vmem(3, planes + 6, rows, width),
        vmem(*consts[0].shape),
        vmem(*consts[1].shape),
        vmem(*consts[2].shape),
        vmem(*consts[3].shape),
        vmem(*consts[4].shape),
        vmem(*consts[5].shape),
        pltpu.VMEM(consts[6].shape, BF16),
        vmem(2, 2 * half),
        vmem(3, planes, depth, 2 * half),
        pltpu.VMEM((width, width), BF16),
        pltpu.VMEM((width, width), BF16),
        pltpu.VMEM((2 * flat, width), BF16),
        pltpu.VMEM((2 * flat, width), BF16),
        vmem(3 * planes, rows, width),
        vmem(3 * planes, rows, width),
        vmem(3 * planes, rows, width),
        wide(3 * planes),
        wide(3 * planes),
        wide(3 * planes),
        wide(3 * planes),
        wide(planes + 6),
        wide(planes + 4),
        wide(planes + 6),
        vmem(depth, 2 * half),
        wide(planes + 2),
        wide(3 * planes),
        vmem(3 * planes, rows, width),
        pltpu.SemaphoreType.DMA((11,)),
        pltpu.SemaphoreType.DMA((8,)),
        pltpu.SemaphoreType.DMA((8,)),
        pltpu.SemaphoreType.DMA((5, GROUPS)),
        pltpu.SemaphoreType.DMA((5, GROUPS)),
        pltpu.SemaphoreType.DMA((3, GROUPS)),
        pltpu.SemaphoreType.DMA((3, GROUPS)),
        pltpu.SemaphoreType.DMA((5,)),
    ]
    call = pl.pallas_call(
        functools.partial(body, slabs),
        out_shape=(
            jax.ShapeDtypeStruct(vel.shape, F32),
            jax.ShapeDtypeStruct(q_old.shape, F32),
            jax.ShapeDtypeStruct(pressure_guess.shape, F32),
        ),
        in_specs=[pl.BlockSpec(memory_space=pltpu.SMEM)] + [any_spec] * 11,
        out_specs=(any_spec, any_spec, any_spec),
        scratch_shapes=scratch,
        compiler_params=pltpu.CompilerParams(
            collective_id=0, has_side_effects=True, vmem_limit_bytes=63 * 2**20
        ),
        name="section",
    )
    return call(shear_shift, vel, q_old, pressure_guess, edge, *consts)


def solution(mesh):
    in_specs = (P(None, "gx", "yz", None), P(None, "gx", None, "yz"), P("gx", None, "yz"), P())
    out_specs = (P(None, "gx", "yz", None), P(None, "gx", None, "yz"), P("gx", None, "yz"))
    return jax.shard_map(
        functools.partial(local, mesh.shape["gx"]),
        mesh=mesh, in_specs=in_specs, out_specs=out_specs, check_vma=False,
    )
```

time: 462 us -> 123 us (0.27); the launches traced: 455 us -> 123 us
  matrix products: 153 us -> 0 us
  Pallas kernels: 0 us -> 115 us
  other arithmetic: 103 us -> 0.63 us
  local copies, waits for them, and re-layouts: 105 us -> 5.3 us
  waiting for transfers between devices: 49.3 us -> 0 us
  starting transfers between devices: 42.2 us -> 0 us
    dot_general x13 -> x0, matrix products: 153 us -> none  [the longest x4 121 us: to_modes(): jnp.dot(flat, forward_y, precision=highest, preferred_element_type=jnp.fl...]
    pallas_call x0 -> x1, Pallas kernels: none -> 115 us  [local(): return call(shear_shift, vel, q_old, pressure_guess, edge, *consts)]
    all_to_all x7 -> x0, waiting for transfers between devices: 37.9 us -> none  [the longest x6 24.6 us: exchange_in_order(): out = lax.all_to_all(out, axes[k], k, k, tiled=True)]
    all_to_all x7 -> x0, starting transfers between devices: 34.3 us -> none  [the longest x6 28.6 us: exchange_in_order(): out = lax.all_to_all(out, axes[k], k, k, tiled=True)]
    mul x16 -> x0, other arithmetic: 31.1 us -> none  [the longest x2 10.6 us: scale_modes(): return join_parts(factor * real_part, factor * imag_part, packed.shape)]
    dot_general x4 -> x0, other arithmetic: 26 us -> none  [the longest x1 19.5 us: local(): jnp.dot(flat, inverse_y, precision=highest, preferred_element_type=jnp.fl...]
    reshape x10 -> x0, local copies, waits for them, and re-layouts: 25.3 us -> none  [the longest x6 19.5 us: join_parts(): return jnp.concatenate([real_part, imag_part], axis=-2).reshape(shape)]
    concatenate x14 -> x0, other arithmetic: 17.3 us -> none  [the longest x8 12.9 us: join_parts(): return jnp.concatenate([real_part, imag_part], axis=-2).reshape(shape)]
  transfers between devices with their start and end apart: 11 -> 0, of which waited for: 5 -> 0; matrix products, arithmetic and copies ran while one was open for 57% -> 0% of each run, Pallas kernels for 0% -> 0%
where the time goes in v1:
time: 123 us
  Pallas kernels  115 us (93%)
  local copies, waits for them, and re-layouts  5.3 us (4%)
  between operations  1.3 us (1%)
    pallas_call x1, Pallas kernels, local(): return call(shear_shift, vel, q_old, pressure_guess, edge, *consts)  115 us
    unnamed x7, local copies, waits for them, and re-layouts  5.3 us

profile of v1, /device:TPU:0, one launch (start us, length us, event | category | flops | bytes accessed | tf_op | source)
XLA Modules:
  0.0 122.6 jit_solution(13624261021791440903)
XLA Ops:
  1.3 0.1 fusion.5
  1.3 0.6 pad_maximum_fusion.edge_hbm
  1.9 115.4 %section.1 = (f32[3,6,24,1024]{3,2,1,0:T(8,128)}, f32[3,6,192,128]{3,2,1,0:T(8,128)}, f32[6,192,128]{2,1,0:T(8,128)}) custom-call(s32[1]{0:T(128)} %copy.17.shift_ref, f32[3,6,24,1024]{3,2,1,0:T(8,128)} %vel_hbm.1, f32[3,6,192,128]{3,2,1,0:T(8,128)} %qold_hbm.1, f32[6,192,128]{2,1,0:T(8,128)} %guess_hbm.1, f32[2,128]{1,0:T(2,128)} %pad_maximum_fusion.edge_hbm, ...), custom_call_target="tpu_custom_call" | custom-call | tf_op jit(solution)/shard_map/section/pallas_call | solution.py:710
  117.3 0.0 copy-start
  117.3 3.0 %copy.18 = f32[3,6,24,1024]{3,2,1,0:T(8,128)} copy(f32[3,6,24,1024]{3,2,1,0:T(8,128)} %get-tuple-element.8) | data formatting | bytes 3538944
  120.3 0.0 copy-done
  120.3 0.0 copy-start.1
  120.3 1.2 copy.19
  121.5 0.3 copy-done.1
  121.8 0.8 copy.20
Async XLA Ops:
  117.3 3.0 %copy-start = (f32[3,6,192,128]{3,2,1,0:T(8,128)S(1)}, f32[3,6,192,128]{3,2,1,0:T(8,128)}, u32[]{:S(2)}) copy-start(f32[3,6,192,128]{3,2,1,0:T(8,128)} %get-tuple-element.9) | copy-start | bytes 5308420
  120.3 1.5 %copy-start.1 = (f32[6,192,128]{2,1,0:T(8,128)S(1)}, f32[6,192,128]{2,1,0:T(8,128)}, u32[]{:S(2)}) copy-start(f32[6,192,128]{2,1,0:T(8,128)} %get-tuple-element.10) | copy-start | bytes 1769476

commit v2 on v1

v2 whole, which is shorter than its diff:
```python
import functools
import math

import jax
import jax.numpy as jnp
import numpy as np
from jax import lax
from jax.experimental import pallas as pl
from jax.experimental.pallas import tpu as pltpu
from jax.sharding import PartitionSpec as P

viscosity = 0.05
time_step = 0.2
keep_weight = -5.0 / 9.0
section_weight = 15.0 / 16.0
shear_param = 1.5
fraction = 0.375
GROUPS = 8
MESH = pl.DeviceIdType.MESH
F32 = jnp.float32
BF16 = jnp.bfloat16


def tables(width_y, depth_z):
    half = width_y // (2 * GROUPS)
    lanes = np.arange(width_y)
    mode = lanes // (2 * half) * half + lanes % half
    is_im = (lanes // half) % 2 == 1
    coarse = np.arange(width_y // half)
    fine = np.arange(half)

    def angle(n, k):
        return 2.0 * np.pi / width_y * ((n[:, None] * k[None, :]) % width_y)

    scale = 1.0 / math.sqrt(width_y)
    alpha = angle(coarse * half, mode)
    beta = angle(fine, mode)
    fwd_coarse = np.concatenate([np.cos(alpha), np.sin(alpha)])
    fwd_fine = scale * np.where(is_im[None], -np.sin(beta), np.cos(beta))
    cells = np.arange(width_y)
    alpha = angle(np.arange(GROUPS) * half, cells)
    beta = angle(fine, cells)
    inv_coarse = np.concatenate([np.cos(alpha), np.sin(alpha)])
    inv_fine = (2.0 * section_weight * scale) * np.stack([np.cos(beta), -np.sin(beta)])
    wave_y = 2.0 * np.pi / width_y * mode[None, :]
    m = np.arange(depth_z)
    signed = np.where(m < depth_z // 2, m, m - depth_z)
    wave_z = (2.0 * np.pi / depth_z * signed)[:, None]
    angle_z = 2.0 * np.pi / depth_z * ((m[:, None] * m[None, :]) % depth_z)
    forward = np.exp(-1j * angle_z) / math.sqrt(depth_z)
    mats = [
        forward,
        1j * wave_z * forward,
        -viscosity * wave_z * wave_z * forward,
        np.exp(1j * angle_z) / math.sqrt(depth_z),
    ]
    stacked = []
    for mat in mats:
        both = np.concatenate([mat.real, mat.imag]).astype(np.float32)
        high = both.astype(BF16)
        low = (both - high.astype(np.float32)).astype(BF16)
        stacked.append(np.concatenate([high, low]))
    as32 = lambda v: jnp.asarray(np.asarray(v, np.float32))
    return (
        as32(fwd_coarse),
        as32(fwd_fine),
        as32(inv_coarse),
        as32(inv_fine),
        as32(wave_y),
        as32(np.broadcast_to(wave_z, (depth_z, 2 * half))),
        jnp.asarray(np.stack(stacked)),
    )


def split(value):
    high = value.astype(BF16)
    low = (value - high.astype(F32)).astype(BF16)
    return high, low


def mm(a, b):
    return jnp.dot(a, b, preferred_element_type=F32)


def body(
    slabs,
    shift_ref,
    vel_hbm,
    qold_hbm,
    guess_hbm,
    edge_hbm,
    fcoarse_hbm,
    ffine_hbm,
    icoarse_hbm,
    ifine_hbm,
    wavey_hbm,
    wavez_hbm,
    zmat_hbm,
    vnext,
    qnext,
    pout,
    ghost,
    fcoarse,
    ffine,
    icoarse,
    ifine,
    wavey,
    wavez,
    zmat,
    edge,
    qold,
    f_hi,
    f_lo,
    left_side,
    spec_u,
    spec_c,
    spec_w,
    got_u,
    got_c,
    got_w,
    tend,
    tend_x,
    cross,
    guess,
    late,
    recip,
    diverge,
    first,
    press,
    spatial,
    got_s,
    load_sem,
    halo_send,
    halo_recv,
    fwd_send,
    fwd_recv,
    inv_send,
    inv_recv,
):
    gx = lax.axis_index("gx")
    me = lax.axis_index("yz")
    my_z = me // 2
    right = lax.rem(gx + 1, slabs)
    left = lax.rem(gx + slabs - 1, slabs)
    planes = 6
    rows = 24
    width = 1024
    depth = 192
    lanes = 128
    half = 64
    flat = planes * rows * 3

    def peer(d):
        return lax.rem(me + d, GROUPS)

    def own_cols(ref_index):
        return pl.ds(pl.multiple_of(ref_index * lanes, lanes), lanes)

    def own_rows(ref_index):
        return pl.ds(pl.multiple_of(ref_index * rows, 8), rows)

    loads = [
        (vel_hbm, ghost.at[:, pl.ds(3, planes)]),
        (fcoarse_hbm, fcoarse),
        (ffine_hbm, ffine.at[0]),
        (guess_hbm, guess.at[pl.ds(2, planes)]),
        (wavey_hbm, wavey),
        (edge_hbm, edge),
        (zmat_hbm, zmat),
        (wavez_hbm, wavez),
        (icoarse_hbm, icoarse),
        (ifine_hbm, ifine),
        (qold_hbm, qold),
    ]
    loads = [pltpu.make_async_copy(s, d, load_sem.at[i]) for i, (s, d) in enumerate(loads)]
    for i in (1, 2, 0, 3, 4, 5, 6, 7, 8, 9, 10):
        loads[i].start()

    barrier = pltpu.get_barrier_semaphore()
    for d in range(1, GROUPS):
        pl.semaphore_signal(
            barrier, inc=1, device_id={"gx": gx, "yz": peer(d)}, device_id_type=MESH
        )
    for side in (left, right):
        pl.semaphore_signal(barrier, inc=1, device_id={"gx": side, "yz": me}, device_id_type=MESH)

    def x_copy(src, dst, slot, target):
        return pltpu.make_async_remote_copy(
            src_ref=src, dst_ref=dst, send_sem=halo_send.at[slot], recv_sem=halo_recv.at[slot],
            device_id={"gx": target, "yz": me}, device_id_type=MESH,
        )

    def halo(ref, count, slot, lead):
        def at(start):
            return ref.at[:, pl.ds(start, count)] if lead else ref.at[pl.ds(start, count)]

        return (
            x_copy(at(count), at(count + planes), slot, left),
            x_copy(at(planes), at(0), slot + 1, right),
        )

    sign = jnp.where(lax.broadcasted_iota(jnp.int32, (1, lanes), 1) < half, -1.0, 1.0).astype(F32)

    def turned(value):
        return pltpu.roll(value, half, 1) * sign

    def store_split(at, value, gap=flat):
        high, low = split(value)
        left_side[pl.ds(pl.multiple_of(at, 48), 48), :] = high
        left_side[pl.ds(pl.multiple_of(at + gap, 48), 48), :] = low

    def build(col):
        cols = pl.ds(col, 256)
        for side in range(2):
            part = pl.ds(pl.multiple_of(col + side * lanes, lanes), lanes)
            ffine[1, :, part] = -turned(ffine[0, :, part])

        def step(a, carry):
            value = (
                fcoarse[pl.ds(a, 1), cols] * ffine[0, :, cols]
                + fcoarse[pl.ds(a + width // half, 1), cols] * ffine[1, :, cols]
            )
            high, low = split(value)
            where = pl.ds(pl.multiple_of(a * half, half), half)
            f_hi[where, cols] = high
            f_lo[where, cols] = low
            return carry

        lax.fori_loop(0, width // half, step, 0)

    def pairs_loop(write):
        def step(i, carry):
            write(i // 3, lax.rem(i, 3) * 2, i * 48)
            return carry

        lax.fori_loop(0, 9, step, 0)

    def to_modes(slot, col):
        cols = pl.ds(col, 256)
        both = mm(left_side[pl.ds(slot * 2 * flat, 2 * flat), :], f_hi[:, cols])
        low = mm(left_side[pl.ds(slot * 2 * flat, flat), :], f_lo[:, cols])
        return both[:flat] + both[flat:] + low

    def column(i):
        target = lax.rem(my_z + 1 + i, 4)
        return target, pl.multiple_of(target * 256, 256)

    def fwd_copy(spec, got, kind, dest, at, count):
        return pltpu.make_async_remote_copy(
            src_ref=spec.at[pl.ds(at, count), :, own_cols(dest)],
            dst_ref=got.at[pl.ds(at, count), own_rows(me), :],
            send_sem=fwd_send.at[kind, dest],
            recv_sem=fwd_recv.at[kind, me],
            device_id={"gx": gx, "yz": dest},
            device_id_type=MESH,
        )

    def fwd_own(spec, got, kind, at, count):
        return pltpu.make_async_copy(
            spec.at[pl.ds(at, count), :, own_cols(me)],
            got.at[pl.ds(at, count), own_rows(me), :],
            fwd_recv.at[kind, me],
        )

    def fwd_wait(spec, got, kind, at, count):
        fwd_own(spec, got, kind, at, count).wait()

        def step(d, carry):
            src = peer(d)
            where = got.at[pl.ds(at, count), own_rows(src), :]
            pltpu.make_async_remote_copy(
                src_ref=where, dst_ref=where, send_sem=fwd_send.at[kind, src],
                recv_sem=fwd_recv.at[kind, src], device_id={"gx": gx, "yz": src},
                device_id_type=MESH,
            ).wait_recv()
            return carry

        lax.fori_loop(1, GROUPS, step, 0)

    def send_column(spec, got, kind, i, at, count):
        target, _ = column(i)
        for side in range(2):
            dest = target * 2 + side

            @pl.when(dest != me)
            def _():
                fwd_copy(spec, got, kind, dest, at, count).start()

    def put_u(c, p, at):
        store_split(at, ghost[c, pl.ds(3 + p, 2)].reshape(48, width))

    def modes_of(spec, i, make):
        _, col = column(i)
        if make:
            build(col)
        spec[:, :, pl.ds(col, 256)] = to_modes(0, col).reshape(18, rows, 256)

    loads[1].wait()
    loads[2].wait()
    loads[0].wait()
    pairs_loop(put_u)
    modes_of(spec_u, 0, True)
    loads[3].wait()
    pl.semaphore_wait(barrier, GROUPS + 1)
    vel_halo = halo(ghost, 3, 0, True)
    guess_halo = halo(guess, 2, 2, False)
    for copy in vel_halo + guess_halo:
        copy.start()
    send_column(spec_u, got_u, 0, 0, 0, 18)

    def rest_u(i, carry):
        modes_of(spec_u, i, True)
        send_column(spec_u, got_u, 0, i, 0, 18)
        return carry

    lax.fori_loop(1, 4, rest_u, 0)
    fwd_own(spec_u, got_u, 0, 0, 18).start()

    def put_c(c, p, at):
        u_z = ghost[2, pl.ds(3 + p, 2)]
        store_split(at, (-u_z * ghost[c, pl.ds(3 + p, 2)]).reshape(48, width))

    pairs_loop(put_c)

    def all_c(i, carry):
        modes_of(spec_c, i, False)
        send_column(spec_c, got_c, 1, i, 0, 18)
        return carry

    lax.fori_loop(0, 4, all_c, 0)
    fwd_own(spec_c, got_c, 1, 0, 18).start()

    for copy in vel_halo:
        copy.wait_recv()
    shift = shift_ref[0]

    def fix(start, amount, extra):
        def step(i, carry):
            c, p = i // 3, lax.rem(i, 3) + start
            once = pltpu.roll(ghost[c, p], amount, 1)
            ghost[c, p] = (1.0 - fraction) * once + fraction * pltpu.roll(once, extra, 1)
            return carry

        lax.fori_loop(0, 9, step, 0)

    @pl.when(gx == 0)
    def _():
        fix(0, lax.rem(width - shift, width), width - 1)

    @pl.when(gx == slabs - 1)
    def _():
        fix(planes + 3, shift, 1)

    total_x = planes * slabs
    omega = 2.0 / total_x

    def put_ab(i, carry):
        c, p = i // 3, lax.rem(i, 3) * 2
        terms_a = []
        terms_b = []
        for q in range(2):
            at = p + q + 3
            u_x = [ghost[0, at + o] for o in range(-3, 4)]
            u_i = [ghost[c, at + o] for o in range(-3, 4)]
            prod = [x * y for x, y in zip(u_x, u_i)]
            slope = (
                (45.0 / 60.0) * (prod[4] - prod[2])
                - (9.0 / 60.0) * (prod[5] - prod[1])
                + (1.0 / 60.0) * (prod[6] - prod[0])
            )
            bend = (
                (2.0 / 180.0) * (u_i[6] + u_i[0])
                - (27.0 / 180.0) * (u_i[5] + u_i[1])
                + (270.0 / 180.0) * (u_i[4] + u_i[2])
                - (490.0 / 180.0) * u_i[3]
            )
            u_y = ghost[1, at]
            weight_y = jnp.where(c == 0, 2.0 * omega, 0.0).astype(F32)
            weight_x = jnp.where(c == 1, -(2.0 - shear_param) * omega, 0.0).astype(F32)
            terms_a.append(viscosity * bend - slope + (weight_y * u_y + weight_x * u_x[3]))
            place = (gx * planes + p + q).astype(F32) + 0.5 - total_x / 2.0
            background = -shear_param * omega * place
            terms_b.append(-(u_y + background) * u_i[3])
        store_split(i * 48, jnp.concatenate(terms_a, axis=0))
        store_split(2 * flat + i * 48, jnp.concatenate(terms_b, axis=0))
        return carry

    lax.fori_loop(0, 9, put_ab, 0)
    loads[4].wait()

    def combine(i, carry):
        _, col = column(i)
        ya = to_modes(0, col)
        yb = to_modes(1, col)
        for side in range(2):
            wide = pl.ds(pl.multiple_of(col + side * lanes, lanes), lanes)
            cut = slice(side * lanes, (side + 1) * lanes)
            ky = wavey[0:1, wide]
            yu = spec_u[:, :, wide].reshape(flat, lanes)
            out = ya[:, cut] + turned(yb[:, cut]) * ky - (viscosity * ky * ky) * yu
            spec_w[:, :, wide] = out.reshape(18, rows, lanes)
        return carry

    lax.fori_loop(0, 4, combine, 0)
    w_parts = ((2, 0, 6), (3, 6, 6), (4, 12, 2), (5, 14, 2), (6, 16, 2))
    for kind, at, count in w_parts:
        def send_w(i, carry, kind=kind, at=at, count=count):
            send_column(spec_w, got_w, kind, i, at, count)
            return carry

        lax.fori_loop(0, 4, send_w, 0)
        fwd_own(spec_w, got_w, kind, at, count).start()

    for i in (5, 6, 7, 8, 9):
        loads[i].wait()
    own_ky = wavey[0:1, own_cols(me)]
    recip[...] = 1.0 / (2.0 + own_ky * own_ky + wavez[...] * wavez[...])

    def build_back(g, carry):
        cosine = icoarse[pl.ds(g, 1), :]
        sine = icoarse[pl.ds(g + GROUPS, 1), :]
        for part in range(2):
            if part == 0:
                value = cosine * ifine[0] + sine * ifine[1]
            else:
                value = cosine * ifine[1] - sine * ifine[0]
            high, low = split(value)
            where = pl.ds(pl.multiple_of(g * lanes + part * half, half), half)
            f_hi[where, :] = high
            f_lo[where, :] = low
        return carry

    lax.fori_loop(0, GROUPS, build_back, 0)
    top = lax.broadcasted_iota(jnp.int32, (16, width), 0) == 0
    for table in (f_hi, f_lo):
        lines = table[0:16, :].astype(F32)
        table[0:16, :] = jnp.where(top, lines * 0.5, lines).astype(BF16)

    cosine = edge[0:1, :]
    sine = edge[1:2, :]

    def rotate_ends(lower, upper):
        @pl.when(gx == 0)
        def _():
            for ref, j in lower:
                value = ref[j]
                ref[j] = value * cosine + turned(value) * sine

        @pl.when(gx == slabs - 1)
        def _():
            for ref, j in upper:
                value = ref[j]
                ref[j] = value * cosine - turned(value) * sine

    for copy in guess_halo:
        copy.wait_recv()
    rotate_ends(((guess, 0), (guess, 1)), ((guess, 8), (guess, 9)))

    def z_pair(ref, at, kind):
        value = jnp.concatenate([ref[at], ref[at + 1]], axis=1)
        high, low = split(value)
        return mm(zmat[kind], high), mm(zmat[kind, pl.ds(0, 2 * depth)], low)

    def z_join(parts):
        total = sum(wide[: 2 * depth] + wide[2 * depth :] + low for wide, low in parts)
        out = []
        for q in range(2):
            cut = slice(q * lanes, (q + 1) * lanes)
            out.append(total[:depth, cut] + turned(total[depth:, cut]))
        return out

    fwd_wait(spec_u, got_u, 0, 0, 18)
    fwd_wait(spec_c, got_c, 1, 0, 18)

    def z_first(i, carry):
        at = i * 2
        values = z_join([z_pair(got_c, at, 1), z_pair(got_u, at, 2)])
        tend[at] = values[0]
        tend[at + 1] = values[1]
        return carry

    lax.fori_loop(0, 9, z_first, 0)

    def z_last(c, pair):
        at = c * planes + pair * 2
        values = z_join([z_pair(got_w, at, 0)])
        for q in range(2):
            value = tend[at + q] + values[q]
            tend[at + q] = value
            values[q] = value
        return values

    fwd_wait(spec_w, got_w, 2, 0, 6)

    def last_x(pair, carry):
        values = z_last(0, pair)
        for q in range(2):
            tend_x[2 * pair + q + 1] = values[q]
        return carry

    lax.fori_loop(0, 3, last_x, 0)
    x_halo = halo(tend_x, 1, 4, False)
    for copy in x_halo:
        copy.start()

    fwd_wait(spec_w, got_w, 3, 6, 6)

    def last_y(pair, carry):
        values = z_last(1, pair)
        for q in range(2):
            cross[2 * pair + q] = turned(values[q]) * own_ky
        return carry

    lax.fori_loop(0, 3, last_y, 0)

    def last_z(pair, carry):
        fwd_wait(spec_w, got_w, 4 + pair, 12 + 2 * pair, 2)
        values = z_last(2, pair)
        for q in range(2):
            j = 2 * pair + q
            cross[j] = cross[j] + turned(values[q]) * wavez[...]
        return carry

    lax.fori_loop(0, 3, last_z, 0)

    def sweep_own(j):
        diverge[j + 1] = 0.5 * (tend_x[j + 2] - tend_x[j]) + cross[j]
        first[j + 1] = (guess[j + 3] + guess[j + 1] - diverge[j + 1]) * recip[...]

    for j in (1, 4):
        sweep_own(j)
    late[0] = 0.5 * tend_x[2] + cross[0]
    late[1] = first[2]
    late[2] = 0.5 * tend_x[5] - cross[5]
    late[3] = first[5]
    late_halo = (
        x_copy(late.at[pl.ds(0, 2)], late.at[pl.ds(6, 2)], 6, left),
        x_copy(late.at[pl.ds(2, 2)], late.at[pl.ds(4, 2)], 7, right),
    )
    for copy in late_halo:
        copy.start()
    for copy in x_halo:
        copy.wait_recv()
    rotate_ends(((tend_x, 0),), ((tend_x, planes + 1),))
    for j in (0, 2, 3, 5):
        sweep_own(j)

    def sweep_again(j):
        press[j + 1] = (first[j + 2] + first[j] - diverge[j + 1]) * recip[...]

    for j in (1, 2, 3, 4):
        sweep_again(j)
    loads[10].wait()

    def inv_copy(pair, c, dest):
        at = pair * 6 + c * 2
        return pltpu.make_async_remote_copy(
            src_ref=spatial.at[pl.ds(at, 2), own_rows(dest), :],
            dst_ref=got_s.at[pl.ds(at, 2), :, own_cols(me)],
            send_sem=inv_send.at[pair * 3 + c, dest],
            recv_sem=inv_recv.at[pair * 3 + c, me],
            device_id={"gx": gx, "yz": dest},
            device_id_type=MESH,
        )

    def inv_own(pair, c):
        at = pair * 6 + c * 2
        return pltpu.make_async_copy(
            spatial.at[pl.ds(at, 2), own_rows(me), :],
            got_s.at[pl.ds(at, 2), :, own_cols(me)],
            inv_recv.at[pair * 3 + c, me],
        )

    def finish(pair):
        for q in range(2):
            p = 2 * pair + q
            here = press[p + 1]
            side = turned(here)
            pout[p] = here
            slopes = (0.5 * (press[p + 2] - press[p]), side * own_ky, side * wavez[...])
            for c in range(3):
                qnext[c, p] = keep_weight * qold[c, p] + time_step * (
                    tend[c * planes + p] - slopes[c]
                )

        def back(c, carry):
            at = pair * 6 + c * 2
            values = z_join([z_pair(qnext.at[c], 2 * pair, 3)])
            spatial[at] = values[0]
            spatial[at + 1] = values[1]

            def send(d, inner):
                inv_copy(pair, c, peer(d)).start()
                return inner

            lax.fori_loop(1, GROUPS, send, 0)
            inv_own(pair, c).start()
            return carry

        lax.fori_loop(0, 3, back, 0)

    finish(1)
    for copy in late_halo:
        copy.wait_recv()
    rotate_ends(((late, 4), (late, 5)), ((late, 6), (late, 7)))
    low = 0.5 * tend_x[1] - late[4]
    first[0] = (guess[2] + guess[0] - low) * recip[...]
    press[0] = (first[1] + late[5] - low) * recip[...]
    high = late[6] - 0.5 * tend_x[6]
    first[7] = (guess[9] + guess[7] - high) * recip[...]
    press[7] = (late[7] + first[6] - high) * recip[...]
    for j in (0, 5):
        sweep_again(j)

    def finish_ends(i, carry):
        finish(i * 2)
        return carry

    lax.fori_loop(0, 2, finish_ends, 0)

    rows_c = planes * rows

    def arrive(i, carry):
        pair = jnp.where(i == 0, 1, jnp.where(i == 1, 0, 2))
        for c in range(3):
            inv_own(pair, c).wait()

            def step(d, inner, c=c):
                src = peer(d)
                where = got_s.at[pl.ds(pair * 6 + c * 2, 2), :, own_cols(src)]
                pltpu.make_async_remote_copy(
                    src_ref=where, dst_ref=where, send_sem=inv_send.at[pair * 3 + c, src],
                    recv_sem=inv_recv.at[pair * 3 + c, src], device_id={"gx": gx, "yz": src},
                    device_id_type=MESH,
                ).wait_recv()
                return inner

            lax.fori_loop(1, GROUPS, step, 0)
        high, low = split(got_s[pl.ds(pair * 6, 6)].reshape(rows_c, width))
        left_side[0:rows_c, :] = high
        left_side[rows_c : 2 * rows_c, :] = low

        def cells(k, inner):
            cols = pl.ds(pl.multiple_of(k * 256, 256), 256)
            both = mm(left_side[0 : 2 * rows_c, :], f_hi[:, cols])
            out = both[:rows_c] + both[rows_c:] + mm(left_side[0:rows_c, :], f_lo[:, cols])
            for c in range(3):
                for q in range(2):
                    at = (c * 2 + q) * rows
                    p = 2 * pair + q
                    vnext[c, p, :, cols] = ghost[c, p + 3, :, cols] + out[at : at + rows]
            return inner

        lax.fori_loop(0, 4, cells, 0)
        return carry

    lax.fori_loop(0, 3, arrive, 0)

    def drain(d, carry):
        dest = peer(d)
        fwd_copy(spec_u, got_u, 0, dest, 0, 18).wait_send()
        fwd_copy(spec_c, got_c, 1, dest, 0, 18).wait_send()
        for kind, at, count in w_parts:
            fwd_copy(spec_w, got_w, kind, dest, at, count).wait_send()
        for pair in range(3):
            for c in range(3):
                inv_copy(pair, c, dest).wait_send()
        return carry

    lax.fori_loop(1, GROUPS, drain, 0)
    for copy in vel_halo + guess_halo + x_halo + late_halo:
        copy.wait_send()


def local(slabs, vel, q_old, pressure_guess, shear_shift):
    width = vel.shape[3]
    depth = q_old.shape[2]
    half = width // (2 * GROUPS)
    planes, rows = vel.shape[1], vel.shape[2]
    consts = tables(width, depth)
    modes = lax.axis_index("yz") * half + jnp.arange(2 * half, dtype=jnp.int32) % half
    angle = (2.0 * math.pi / width) * (
        (modes * shear_shift[0] % width).astype(F32) + fraction * modes.astype(F32)
    )
    edge = jnp.stack([jnp.cos(angle), jnp.sin(angle)])
    any_spec = pl.BlockSpec(memory_space=pl.ANY)
    vmem = lambda *shape: pltpu.VMEM(shape, F32)
    wide = lambda n: pltpu.VMEM((n, depth, 2 * half), F32)
    flat = 3 * planes * rows
    scratch = [
        vmem(3, planes + 6, rows, width),
        vmem(*consts[0].shape),
        vmem(2, *consts[1].shape),
        vmem(*consts[2].shape),
        vmem(*consts[3].shape),
        vmem(*consts[4].shape),
        vmem(*consts[5].shape),
        pltpu.VMEM(consts[6].shape, BF16),
        vmem(2, 2 * half),
        vmem(3, planes, depth, 2 * half),
        pltpu.VMEM((width, width), BF16),
        pltpu.VMEM((width, width), BF16),
        pltpu.VMEM((4 * flat, width), BF16),
        vmem(3 * planes, rows, width),
        vmem(3 * planes, rows, width),
        vmem(3 * planes, rows, width),
        wide(3 * planes),
        wide(3 * planes),
        wide(3 * planes),
        wide(3 * planes),
        wide(planes + 2),
        wide(planes),
        wide(planes + 4),
        wide(8),
        vmem(depth, 2 * half),
        wide(planes + 2),
        wide(planes + 2),
        wide(planes + 2),
        wide(3 * planes),
        vmem(3 * planes, rows, width),
        pltpu.SemaphoreType.DMA((11,)),
        pltpu.SemaphoreType.DMA((8,)),
        pltpu.SemaphoreType.DMA((8,)),
        pltpu.SemaphoreType.DMA((7, GROUPS)),
        pltpu.SemaphoreType.DMA((7, GROUPS)),
        pltpu.SemaphoreType.DMA((9, GROUPS)),
        pltpu.SemaphoreType.DMA((9, GROUPS)),
    ]
    call = pl.pallas_call(
        functools.partial(body, slabs),
        out_shape=(
            jax.ShapeDtypeStruct(vel.shape, F32),
            jax.ShapeDtypeStruct(q_old.shape, F32),
            jax.ShapeDtypeStruct(pressure_guess.shape, F32),
        ),
        in_specs=[pl.BlockSpec(memory_space=pltpu.SMEM)] + [any_spec] * 11,
        out_specs=(pl.BlockSpec(memory_space=pltpu.VMEM),) * 3,
        scratch_shapes=scratch,
        compiler_params=pltpu.CompilerParams(
            collective_id=0, has_side_effects=True, vmem_limit_bytes=48 * 2**20
        ),
        name="section",
    )
    return call(shear_shift, vel, q_old, pressure_guess, edge, *consts)


def solution(mesh):
    in_specs = (P(None, "gx", "yz", None), P(None, "gx", None, "yz"), P("gx", None, "yz"), P())
    out_specs = (P(None, "gx", "yz", None), P(None, "gx", None, "yz"), P("gx", None, "yz"))
    return jax.shard_map(
        functools.partial(local, mesh.shape["gx"]),
        mesh=mesh, in_specs=in_specs, out_specs=out_specs, check_vma=False,
    )
```

time: 123 us -> 124 us (level)
  local copies, waits for them, and re-layouts: 5.3 us -> 11.9 us
  Pallas kernels: 115 us -> 111 us
    unnamed x7 -> x21, local copies, waits for them, and re-layouts: 5.3 us -> 11.9 us
    pallas_call x1, Pallas kernels: 115 us -> 111 us  [local(): return call(shear_shift, vel, q_old, pressure_guess, edge, *consts)]
where the time goes in v2:
time: 124 us
  Pallas kernels  111 us (90%)
  local copies, waits for them, and re-layouts  11.9 us (10%)
  between operations  1.32 us (1%)
    pallas_call x1, Pallas kernels, local(): return call(shear_shift, vel, q_old, pressure_guess, edge, *consts)  111 us
    unnamed x21, local copies, waits for them, and re-layouts  11.9 us

profile of v2, /device:TPU:0, one launch (start us, length us, event | category | flops | bytes accessed | tf_op | source)
XLA Modules:
  0.0 124.0 jit_solution(12867895060466692121)
XLA Ops:
  1.3 0.1 fusion.5
  1.3 0.0 copy-start
  1.4 1.4 %copy-done = bf16[4,768,192]{2,1,0:T(8,128)(2,1)S(1)} copy-done((bf16[4,768,192]{2,1,0:T(8,128)(2,1)S(1)}, bf16[4,768,192]{2,1,0:T(8,128)(2,1)}, u32[]{:S(2)}) %copy-start) | copy-done | bytes 1179672
  2.8 0.0 copy-start.1
  2.8 1.1 copy-done.1
  3.8 0.0 copy-start.2
  3.8 1.0 copy-done.2
  4.9 0.0 copy-start.3
  4.9 0.9 copy-done.3
  5.8 0.0 copy-start.4
  5.8 0.9 copy-done.4
  6.7 0.0 copy-start.5
  6.7 0.9 copy-done.5
  7.6 0.0 copy-start.6
  7.6 0.8 copy-done.6
  8.5 0.0 copy-start.7
  8.5 0.7 copy-done.7
  9.1 110.7 %section.1 = (f32[3,6,24,1024]{3,2,1,0:T(8,128)S(1)}, f32[3,6,192,128]{3,2,1,0:T(8,128)}, f32[6,192,128]{2,1,0:T(8,128)S(1)}) custom-call(s32[1]{0:T(128)} %copy.17.shift_ref, f32[3,6,24,1024]{3,2,1,0:T(8,128)} %vel_hbm.1, f32[3,6,192,128]{3,2,1,0:T(8,128)} %qold_hbm.1, f32[6,192,128]{2,1,0:T(8,128)S(1)} %copy-done.1, ...), custom_call_target="tpu_custom_call" | custom-call | tf_op jit(solution)/shard_map/section/pallas_call | solution.py:744
  119.9 0.0 copy-start.8
  119.9 1.2 copy.18
  121.1 0.9 copy-done.8
  122.0 1.2 copy.19
  123.2 0.8 copy.20
  (1 shorter events, 0.0 us)
Async XLA Ops:
  1.3 1.4 %copy-start = (bf16[4,768,192]{2,1,0:T(8,128)(2,1)S(1)}, bf16[4,768,192]{2,1,0:T(8,128)(2,1)}, u32[]{:S(2)}) copy-start(bf16[4,768,192]{2,1,0:T(8,128)(2,1)} %constant.55.clone.zmat_hbm) | copy-start | bytes 3538948
  2.8 1.1 copy-start.1
  3.8 1.0 copy-start.2
  4.9 0.9 copy-start.3
  5.8 0.9 copy-start.4
  6.7 0.9 copy-start.5
  7.6 0.8 copy-start.6
  8.5 0.7 copy-start.7
  119.9 2.1 %copy-start.8 = (f32[3,6,192,128]{3,2,1,0:T(8,128)S(1)}, f32[3,6,192,128]{3,2,1,0:T(8,128)}, u32[]{:S(2)}) copy-start(f32[3,6,192,128]{3,2,1,0:T(8,128)} %get-tuple-element.9) | copy-start | bytes 5308420

commit v3 on v2

--- a/solution.py
+++ b/solution.py
@@ -96,10 +96,11 @@
     wavey_hbm,
     wavez_hbm,
     zmat_hbm,
-    vnext,
-    qnext,
-    pout,
+    vnext_hbm,
+    qnext_hbm,
+    pout_hbm,
     ghost,
+    relay,
     fcoarse,
     ffine,
     icoarse,
@@ -136,12 +137,15 @@
     fwd_recv,
     inv_send,
     inv_recv,
+    out_sem,
 ):
     gx = lax.axis_index("gx")
     me = lax.axis_index("yz")
     my_z = me // 2
     right = lax.rem(gx + 1, slabs)
     left = lax.rem(gx + slabs - 1, slabs)
+    relayed = slabs == 16
+    near = 384
     planes = 6
     rows = 24
     width = 1024
@@ -183,6 +187,22 @@
         )
     for side in (left, right):
         pl.semaphore_signal(barrier, inc=1, device_id={"gx": side, "yz": me}, device_id_type=MESH)
+    place = lax.rem(gx, 8)
+    ends_right = place == 7
+    ends_left = place == 0
+    helps_left = place == 3
+    helps_right = place == 4
+    helper = ends_right | ends_left | helps_left | helps_right
+    far_side = lax.rem(gx + jnp.where(ends_right | helps_left, 5, slabs - 5), slabs)
+    near_side = lax.rem(gx + jnp.where(ends_right | helps_right, slabs - 4, 4), slabs)
+    if relayed:
+
+        @pl.when(helper)
+        def _():
+            for side in (far_side, near_side):
+                pl.semaphore_signal(
+                    barrier, inc=1, device_id={"gx": side, "yz": me}, device_id_type=MESH
+                )
 
     def x_copy(src, dst, slot, target):
         return pltpu.make_async_remote_copy(
@@ -301,10 +321,44 @@
     pairs_loop(put_u)
     modes_of(spec_u, 0, True)
     loads[3].wait()
-    pl.semaphore_wait(barrier, GROUPS + 1)
     vel_halo = halo(ghost, 3, 0, True)
     guess_halo = halo(guess, 2, 2, False)
-    for copy in vel_halo + guess_halo:
+
+    def part(ref, start, side):
+        cols = pl.ds(0, near) if side == 0 else pl.ds(near, width - near)
+        return ref.at[:, pl.ds(start, 3), :, cols]
+
+    near_halo = (
+        x_copy(part(ghost, 3, 0), part(ghost, planes + 3, 0), 0, left),
+        x_copy(part(ghost, planes, 0), part(ghost, 0, 0), 1, right),
+    )
+    to_relay = (
+        x_copy(part(ghost, 3, 1), relay, 8, far_side),
+        x_copy(part(ghost, planes, 1), relay, 8, far_side),
+    )
+    from_relay = (
+        x_copy(relay, part(ghost, planes + 3, 1), 9, near_side),
+        x_copy(relay, part(ghost, 0, 1), 9, near_side),
+    )
+
+    if relayed:
+        pl.semaphore_wait(barrier, jnp.where(helper, GROUPS + 3, GROUPS + 1))
+        for i, ends in ((0, ends_left), (1, ends_right)):
+
+            @pl.when(ends)
+            def _():
+                to_relay[i].start()
+                near_halo[i].start()
+
+            @pl.when(jnp.logical_not(ends))
+            def _():
+                vel_halo[i].start()
+
+    else:
+        pl.semaphore_wait(barrier, GROUPS + 1)
+        for copy in vel_halo:
+            copy.start()
+    for copy in guess_halo:
         copy.start()
     send_column(spec_u, got_u, 0, 0, 0, 18)
 
@@ -330,8 +384,28 @@
     lax.fori_loop(0, 4, all_c, 0)
     fwd_own(spec_c, got_c, 1, 0, 18).start()
 
-    for copy in vel_halo:
-        copy.wait_recv()
+    if relayed:
+        for i, helps in ((0, helps_left), (1, helps_right)):
+
+            @pl.when(helps)
+            def _():
+                to_relay[i].wait_recv()
+                from_relay[i].start()
+
+        for i, ends in ((0, ends_right), (1, ends_left)):
+
+            @pl.when(ends)
+            def _():
+                near_halo[i].wait_recv()
+                from_relay[i].wait_recv()
+
+            @pl.when(jnp.logical_not(ends))
+            def _():
+                vel_halo[i].wait_recv()
+
+    else:
+        for copy in vel_halo:
+            copy.wait_recv()
     shift = shift_ref[0]
 
     def fix(start, amount, extra):
@@ -576,16 +650,15 @@
             p = 2 * pair + q
             here = press[p + 1]
             side = turned(here)
-            pout[p] = here
             slopes = (0.5 * (press[p + 2] - press[p]), side * own_ky, side * wavez[...])
             for c in range(3):
-                qnext[c, p] = keep_weight * qold[c, p] + time_step * (
+                qold[c, p] = keep_weight * qold[c, p] + time_step * (
                     tend[c * planes + p] - slopes[c]
                 )
 
         def back(c, carry):
             at = pair * 6 + c * 2
-            values = z_join([z_pair(qnext.at[c], 2 * pair, 3)])
+            values = z_join([z_pair(qold.at[c], 2 * pair, 3)])
             spatial[at] = values[0]
             spatial[at + 1] = values[1]
 
@@ -618,6 +691,25 @@
 
     lax.fori_loop(0, 2, finish_ends, 0)
 
+    def result(c, pair, slot):
+        return pltpu.make_async_copy(
+            spec_u.at[pl.ds(pair * 6 + 2 * c, 2)], vnext_hbm.at[c, pl.ds(2 * pair, 2)], out_sem.at[slot]
+        )
+
+    results = [
+        pltpu.make_async_copy(press.at[pl.ds(1, planes)], pout_hbm, out_sem.at[0]),
+        pltpu.make_async_copy(qold, qnext_hbm, out_sem.at[1]),
+    ]
+    for copy in results:
+        copy.start()
+    results += [result(c, pair, 2 + pair * 3 + c) for pair in range(3) for c in range(3)]
+
+    def sent_u(d, carry):
+        fwd_copy(spec_u, got_u, 0, peer(d), 0, 18).wait_send()
+        return carry
+
+    lax.fori_loop(1, GROUPS, sent_u, 0)
+
     rows_c = planes * rows
 
     def arrive(i, carry):
@@ -648,17 +740,20 @@
                 for q in range(2):
                     at = (c * 2 + q) * rows
                     p = 2 * pair + q
-                    vnext[c, p, :, cols] = ghost[c, p + 3, :, cols] + out[at : at + rows]
+                    spec_u[pair * 6 + 2 * c + q, :, cols] = (
+                        ghost[c, p + 3, :, cols] + out[at : at + rows]
+                    )
             return inner
 
         lax.fori_loop(0, 4, cells, 0)
+        for c in range(3):
+            result(c, pair, 2 + pair * 3 + c).start()
         return carry
 
     lax.fori_loop(0, 3, arrive, 0)
 
     def drain(d, carry):
         dest = peer(d)
-        fwd_copy(spec_u, got_u, 0, dest, 0, 18).wait_send()
         fwd_copy(spec_c, got_c, 1, dest, 0, 18).wait_send()
         for kind, at, count in w_parts:
             fwd_copy(spec_w, got_w, kind, dest, at, count).wait_send()
@@ -668,8 +763,47 @@
         return carry
 
     lax.fori_loop(1, GROUPS, drain, 0)
-    for copy in vel_halo + guess_halo + x_halo + late_halo:
+    if relayed:
+        for i, ends, helps in ((0, ends_left, helps_left), (1, ends_right, helps_right)):
+
+            @pl.when(ends)
+            def _():
+                to_relay[i].wait_send()
+                near_halo[i].wait_send()
+
+            @pl.when(jnp.logical_not(ends))
+            def _():
+                vel_halo[i].wait_send()
+
+            @pl.when(helps)
+            def _():
+                from_relay[i].wait_send()
+
+    else:
+        for copy in vel_halo:
+            copy.wait_send()
+    for copy in guess_halo + x_halo + late_halo:
         copy.wait_send()
+    for copy in results:
+        copy.wait()
+
+
+def move(*refs):
+    v_in, q_in, p_in, v_out, q_out, p_out, v, q, p, sem_in, sem_out = refs
+    legs = []
+    for c in range(3):
+        legs.append((v_in.at[c], v.at[c], v_out.at[c]))
+        legs.append((q_in.at[c], q.at[c], q_out.at[c]))
+    legs.append((p_in, p, p_out))
+    into = [pltpu.make_async_copy(a, b, sem_in.at[i]) for i, (a, b, _) in enumerate(legs)]
+    out = [pltpu.make_async_copy(b, c, sem_out.at[i]) for i, (_, b, c) in enumerate(legs)]
+    for copy in into:
+        copy.start()
+    for first, second in zip(into, out):
+        first.wait()
+        second.start()
+    for copy in out:
+        copy.wait()
 
 
 def local(slabs, vel, q_old, pressure_guess, shear_shift):
@@ -689,6 +823,7 @@
     flat = 3 * planes * rows
     scratch = [
         vmem(3, planes + 6, rows, width),
+        vmem(3, 3, rows, width - 384),
         vmem(*consts[0].shape),
         vmem(2, *consts[1].shape),
         vmem(*consts[2].shape),
@@ -719,12 +854,13 @@
         wide(3 * planes),
         vmem(3 * planes, rows, width),
         pltpu.SemaphoreType.DMA((11,)),
-        pltpu.SemaphoreType.DMA((8,)),
-        pltpu.SemaphoreType.DMA((8,)),
+        pltpu.SemaphoreType.DMA((10,)),
+        pltpu.SemaphoreType.DMA((10,)),
         pltpu.SemaphoreType.DMA((7, GROUPS)),
         pltpu.SemaphoreType.DMA((7, GROUPS)),
         pltpu.SemaphoreType.DMA((9, GROUPS)),
         pltpu.SemaphoreType.DMA((9, GROUPS)),
+        pltpu.SemaphoreType.DMA((11,)),
     ]
     call = pl.pallas_call(
         functools.partial(body, slabs),
@@ -734,14 +870,24 @@
             jax.ShapeDtypeStruct(pressure_guess.shape, F32),
         ),
         in_specs=[pl.BlockSpec(memory_space=pltpu.SMEM)] + [any_spec] * 11,
-        out_specs=(pl.BlockSpec(memory_space=pltpu.VMEM),) * 3,
+        out_specs=(any_spec, any_spec, any_spec),
         scratch_shapes=scratch,
         compiler_params=pltpu.CompilerParams(
-            collective_id=0, has_side_effects=True, vmem_limit_bytes=48 * 2**20
+            collective_id=0, has_side_effects=True, vmem_limit_bytes=63 * 2**20
         ),
         name="section",
     )
-    return call(shear_shift, vel, q_old, pressure_guess, edge, *consts)
+    out = call(shear_shift, vel, q_old, pressure_guess, edge, *consts)
+    return pl.pallas_call(
+        move,
+        out_shape=tuple(jax.ShapeDtypeStruct(v.shape, F32) for v in out),
+        in_specs=[any_spec] * 3,
+        out_specs=(any_spec, any_spec, any_spec),
+        scratch_shapes=[pltpu.VMEM(v.shape, F32) for v in out]
+        + [pltpu.SemaphoreType.DMA((7,)), pltpu.SemaphoreType.DMA((7,))],
+        compiler_params=pltpu.CompilerParams(vmem_limit_bytes=63 * 2**20),
+        name="move",
+    )(*out)
 
 
 def solution(mesh):

time: 124 us -> 110 us (0.89)
  local copies, waits for them, and re-layouts: 11.9 us -> 0 us
  Pallas kernels: 111 us -> 108 us
    unnamed x21 -> x0, local copies, waits for them, and re-layouts: 11.9 us -> none
    pallas_call x1 -> x2, Pallas kernels: 111 us -> 108 us  [the longest x1 104 us: local(): out = call(shear_shift, vel, q_old, pressure_guess, edge, *consts)]
where the time goes in v3:
time: 110 us
  Pallas kernels  108 us (98%)
  between operations  1.29 us (1%)
    pallas_call x1, Pallas kernels, local(): out = call(shear_shift, vel, q_old, pressure_guess, edge, *consts)  104 us
    pallas_call x1, Pallas kernels, local(): pl.pallas_call(move, out_shape=tuple((jax.ShapeDtypeStruct(v.shape, F32)...  3.47 us

profile of v3, /device:TPU:0, one launch (start us, length us, event | category | flops | bytes accessed | tf_op | source)
XLA Modules:
  0.0 109.7 jit_solution(11689654245275331239)
XLA Ops:
  1.3 0.1 fusion.5
  1.3 0.6 pad_maximum_fusion.edge_hbm
  1.9 104.3 %section.1 = (f32[3,6,24,1024]{3,2,1,0:T(8,128)}, f32[3,6,192,128]{3,2,1,0:T(8,128)}, f32[6,192,128]{2,1,0:T(8,128)}) custom-call(s32[1]{0:T(128)} %copy.14.shift_ref, f32[3,6,24,1024]{3,2,1,0:T(8,128)} %vel_hbm.1, f32[3,6,192,128]{3,2,1,0:T(8,128)} %qold_hbm.1, f32[6,192,128]{2,1,0:T(8,128)} %guess_hbm.1, f32[2,128]{1,0:T(2,128)} %pad_maximum_fusion.edge_hbm, ...), custom_call_target="tpu_custom_call" | custom-call | tf_op jit(solution)/shard_map/section/pallas_call | solution.py:880
  106.2 3.5 %move.1 = (f32[3,6,24,1024]{3,2,1,0:T(8,128)}, f32[3,6,192,128]{3,2,1,0:T(8,128)}, f32[6,192,128]{2,1,0:T(8,128)}) custom-call(f32[3,6,24,1024]{3,2,1,0:T(8,128)} %get-tuple-element.6.refs_0_, f32[3,6,192,128]{3,2,1,0:T(8,128)} %get-tuple-element.7.refs_1_, f32[6,192,128]{2,1,0:T(8,128)} %get-tuple-element.8.refs_2_), custom_call_target="tpu_custom_call" | custom-call | tf_op jit(solution)/shard_map/move/pallas_call | solution.py:881

commit v4 on v3

--- a/solution.py
+++ b/solution.py
@@ -88,7 +88,8 @@
     vel_hbm,
     qold_hbm,
     guess_hbm,
-    edge_hbm,
+    cos_hbm,
+    sin_hbm,
     fcoarse_hbm,
     ffine_hbm,
     icoarse_hbm,
@@ -167,9 +168,10 @@
         (vel_hbm, ghost.at[:, pl.ds(3, planes)]),
         (fcoarse_hbm, fcoarse),
         (ffine_hbm, ffine.at[0]),
-        (guess_hbm, guess.at[pl.ds(2, planes)]),
+        (guess_hbm, guess.at[pl.ds(1, planes)]),
         (wavey_hbm, wavey),
-        (edge_hbm, edge),
+        (cos_hbm, edge.at[0]),
+        (sin_hbm, edge.at[1]),
         (zmat_hbm, zmat),
         (wavez_hbm, wavez),
         (icoarse_hbm, icoarse),
@@ -177,7 +179,7 @@
         (qold_hbm, qold),
     ]
     loads = [pltpu.make_async_copy(s, d, load_sem.at[i]) for i, (s, d) in enumerate(loads)]
-    for i in (1, 2, 0, 3, 4, 5, 6, 7, 8, 9, 10):
+    for i in (1, 2, 0, 3, 4, 5, 6, 7, 8, 9, 10, 11):
         loads[i].start()
 
     barrier = pltpu.get_barrier_semaphore()
@@ -262,7 +264,7 @@
         return both[:flat] + both[flat:] + low
 
     def column(i):
-        target = lax.rem(my_z + 1 + i, 4)
+        target = lax.rem(my_z + jnp.where(i == 0, 1, jnp.where(i == 1, 3, jnp.where(i == 2, 2, 0))), 4)
         return target, pl.multiple_of(target * 256, 256)
 
     def fwd_copy(spec, got, kind, dest, at, count):
@@ -317,12 +319,13 @@
 
     loads[1].wait()
     loads[2].wait()
+    build(column(0)[1])
     loads[0].wait()
     pairs_loop(put_u)
-    modes_of(spec_u, 0, True)
+    modes_of(spec_u, 0, False)
     loads[3].wait()
     vel_halo = halo(ghost, 3, 0, True)
-    guess_halo = halo(guess, 2, 2, False)
+    guess_halo = halo(guess, 1, 2, False)
 
     def part(ref, start, side):
         cols = pl.ds(0, near) if side == 0 else pl.ds(near, width - near)
@@ -485,7 +488,7 @@
         lax.fori_loop(0, 4, send_w, 0)
         fwd_own(spec_w, got_w, kind, at, count).start()
 
-    for i in (5, 6, 7, 8, 9):
+    for i in (5, 6, 7, 8, 9, 10):
         loads[i].wait()
     own_ky = wavey[0:1, own_cols(me)]
     recip[...] = 1.0 / (2.0 + own_ky * own_ky + wavez[...] * wavez[...])
@@ -510,8 +513,8 @@
         lines = table[0:16, :].astype(F32)
         table[0:16, :] = jnp.where(top, lines * 0.5, lines).astype(BF16)
 
-    cosine = edge[0:1, :]
-    sine = edge[1:2, :]
+    cosine = edge[0]
+    sine = edge[1]
 
     def rotate_ends(lower, upper):
         @pl.when(gx == 0)
@@ -528,7 +531,7 @@
 
     for copy in guess_halo:
         copy.wait_recv()
-    rotate_ends(((guess, 0), (guess, 1)), ((guess, 8), (guess, 9)))
+    rotate_ends(((guess, 0),), ((guess, planes + 1),))
 
     def z_pair(ref, at, kind):
         value = jnp.concatenate([ref[at], ref[at + 1]], axis=1)
@@ -599,14 +602,16 @@
 
     def sweep_own(j):
         diverge[j + 1] = 0.5 * (tend_x[j + 2] - tend_x[j]) + cross[j]
-        first[j + 1] = (guess[j + 3] + guess[j + 1] - diverge[j + 1]) * recip[...]
+        first[j + 1] = (guess[j + 2] + guess[j] - diverge[j + 1]) * recip[...]
 
     for j in (1, 4):
         sweep_own(j)
-    late[0] = 0.5 * tend_x[2] + cross[0]
-    late[1] = first[2]
-    late[2] = 0.5 * tend_x[5] - cross[5]
-    late[3] = first[5]
+    low = 0.5 * tend_x[2] + cross[0]
+    high = 0.5 * tend_x[5] - cross[5]
+    late[0] = guess[2] - low
+    late[1] = first[2] - low
+    late[2] = guess[5] + high
+    late[3] = first[5] + high
     late_halo = (
         x_copy(late.at[pl.ds(0, 2)], late.at[pl.ds(6, 2)], 6, left),
         x_copy(late.at[pl.ds(2, 2)], late.at[pl.ds(4, 2)], 7, right),
@@ -624,7 +629,7 @@
 
     for j in (1, 2, 3, 4):
         sweep_again(j)
-    loads[10].wait()
+    loads[11].wait()
 
     def inv_copy(pair, c, dest):
         at = pair * 6 + c * 2
@@ -676,12 +681,12 @@
     for copy in late_halo:
         copy.wait_recv()
     rotate_ends(((late, 4), (late, 5)), ((late, 6), (late, 7)))
-    low = 0.5 * tend_x[1] - late[4]
-    first[0] = (guess[2] + guess[0] - low) * recip[...]
+    low = 0.5 * tend_x[1]
+    first[0] = (guess[1] + late[4] - low) * recip[...]
     press[0] = (first[1] + late[5] - low) * recip[...]
-    high = late[6] - 0.5 * tend_x[6]
-    first[7] = (guess[9] + guess[7] - high) * recip[...]
-    press[7] = (late[7] + first[6] - high) * recip[...]
+    high = 0.5 * tend_x[6]
+    first[7] = (guess[6] + late[6] + high) * recip[...]
+    press[7] = (first[6] + late[7] + high) * recip[...]
     for j in (0, 5):
         sweep_again(j)
 
@@ -710,25 +715,26 @@
 
     lax.fori_loop(1, GROUPS, sent_u, 0)
 
-    rows_c = planes * rows
+    rows_c = 2 * rows
 
     def arrive(i, carry):
-        pair = jnp.where(i == 0, 1, jnp.where(i == 1, 0, 2))
-        for c in range(3):
-            inv_own(pair, c).wait()
-
-            def step(d, inner, c=c):
-                src = peer(d)
-                where = got_s.at[pl.ds(pair * 6 + c * 2, 2), :, own_cols(src)]
-                pltpu.make_async_remote_copy(
-                    src_ref=where, dst_ref=where, send_sem=inv_send.at[pair * 3 + c, src],
-                    recv_sem=inv_recv.at[pair * 3 + c, src], device_id={"gx": gx, "yz": src},
-                    device_id_type=MESH,
-                ).wait_recv()
-                return inner
-
-            lax.fori_loop(1, GROUPS, step, 0)
-        high, low = split(got_s[pl.ds(pair * 6, 6)].reshape(rows_c, width))
+        c = lax.rem(i, 3)
+        pair = jnp.where(i < 3, 1, jnp.where(i < 6, 0, 2))
+        at = pair * 6 + c * 2
+        inv_own(pair, c).wait()
+
+        def step(d, inner):
+            src = peer(d)
+            where = got_s.at[pl.ds(at, 2), :, own_cols(src)]
+            pltpu.make_async_remote_copy(
+                src_ref=where, dst_ref=where, send_sem=inv_send.at[pair * 3 + c, src],
+                recv_sem=inv_recv.at[pair * 3 + c, src], device_id={"gx": gx, "yz": src},
+                device_id_type=MESH,
+            ).wait_recv()
+            return inner
+
+        lax.fori_loop(1, GROUPS, step, 0)
+        high, low = split(got_s[pl.ds(at, 2)].reshape(rows_c, width))
         left_side[0:rows_c, :] = high
         left_side[rows_c : 2 * rows_c, :] = low
 
@@ -736,21 +742,16 @@
             cols = pl.ds(pl.multiple_of(k * 256, 256), 256)
             both = mm(left_side[0 : 2 * rows_c, :], f_hi[:, cols])
             out = both[:rows_c] + both[rows_c:] + mm(left_side[0:rows_c, :], f_lo[:, cols])
-            for c in range(3):
-                for q in range(2):
-                    at = (c * 2 + q) * rows
-                    p = 2 * pair + q
-                    spec_u[pair * 6 + 2 * c + q, :, cols] = (
-                        ghost[c, p + 3, :, cols] + out[at : at + rows]
-                    )
+            spec_u[pl.ds(at, 2), :, cols] = (
+                ghost[c, pl.ds(3 + 2 * pair, 2), :, cols] + out.reshape(2, rows, 256)
+            )
             return inner
 
         lax.fori_loop(0, 4, cells, 0)
-        for c in range(3):
-            result(c, pair, 2 + pair * 3 + c).start()
-        return carry
-
-    lax.fori_loop(0, 3, arrive, 0)
+        result(c, pair, 2 + pair * 3 + c).start()
+        return carry
+
+    lax.fori_loop(0, 9, arrive, 0)
 
     def drain(d, carry):
         dest = peer(d)
@@ -816,7 +817,7 @@
     angle = (2.0 * math.pi / width) * (
         (modes * shear_shift[0] % width).astype(F32) + fraction * modes.astype(F32)
     )
-    edge = jnp.stack([jnp.cos(angle), jnp.sin(angle)])
+    edge = (jnp.cos(angle)[None], jnp.sin(angle)[None])
     any_spec = pl.BlockSpec(memory_space=pl.ANY)
     vmem = lambda *shape: pltpu.VMEM(shape, F32)
     wide = lambda n: pltpu.VMEM((n, depth, 2 * half), F32)
@@ -831,7 +832,7 @@
         vmem(*consts[4].shape),
         vmem(*consts[5].shape),
         pltpu.VMEM(consts[6].shape, BF16),
-        vmem(2, 2 * half),
+        vmem(2, 1, 2 * half),
         vmem(3, planes, depth, 2 * half),
         pltpu.VMEM((width, width), BF16),
         pltpu.VMEM((width, width), BF16),
@@ -845,7 +846,7 @@
         wide(3 * planes),
         wide(planes + 2),
         wide(planes),
-        wide(planes + 4),
+        wide(planes + 2),
         wide(8),
         vmem(depth, 2 * half),
         wide(planes + 2),
@@ -853,7 +854,7 @@
         wide(planes + 2),
         wide(3 * planes),
         vmem(3 * planes, rows, width),
-        pltpu.SemaphoreType.DMA((11,)),
+        pltpu.SemaphoreType.DMA((12,)),
         pltpu.SemaphoreType.DMA((10,)),
         pltpu.SemaphoreType.DMA((10,)),
         pltpu.SemaphoreType.DMA((7, GROUPS)),
@@ -869,7 +870,7 @@
             jax.ShapeDtypeStruct(q_old.shape, F32),
             jax.ShapeDtypeStruct(pressure_guess.shape, F32),
         ),
-        in_specs=[pl.BlockSpec(memory_space=pltpu.SMEM)] + [any_spec] * 11,
+        in_specs=[pl.BlockSpec(memory_space=pltpu.SMEM)] + [any_spec] * 12,
         out_specs=(any_spec, any_spec, any_spec),
         scratch_shapes=scratch,
         compiler_params=pltpu.CompilerParams(
@@ -877,7 +878,7 @@
         ),
         name="section",
     )
-    out = call(shear_shift, vel, q_old, pressure_guess, edge, *consts)
+    out = call(shear_shift, vel, q_old, pressure_guess, *edge, *consts)
     return pl.pallas_call(
         move,
         out_shape=tuple(jax.ShapeDtypeStruct(v.shape, F32) for v in out),

time: 110 us -> 108 us (0.982)
  Pallas kernels: 108 us -> 106 us
    pallas_call x1, Pallas kernels: 104 us -> 102 us  [local(): out = call(shear_shift, vel, q_old, pressure_guess, *edge, *consts)]
where the time goes in v4:
time: 108 us
  Pallas kernels  106 us (98%)
  between operations  1.29 us (1%)
    pallas_call x1, Pallas kernels, local(): out = call(shear_shift, vel, q_old, pressure_guess, *edge, *consts)  102 us
    pallas_call x1, Pallas kernels, local(): pl.pallas_call(move, out_shape=tuple((jax.ShapeDtypeStruct(v.shape, F32)...  3.47 us

profile of v4, /device:TPU:0, one launch (start us, length us, event | category | flops | bytes accessed | tf_op | source)
XLA Modules:
  0.0 107.6 jit_solution(2785526231490757065)
XLA Ops:
  1.3 0.6 fusion.5
  1.9 102.3 %section.1 = (f32[3,6,24,1024]{3,2,1,0:T(8,128)}, f32[3,6,192,128]{3,2,1,0:T(8,128)}, f32[6,192,128]{2,1,0:T(8,128)}) custom-call(s32[1]{0:T(128)} %copy.14.shift_ref, f32[3,6,24,1024]{3,2,1,0:T(8,128)} %vel_hbm.1, f32[3,6,192,128]{3,2,1,0:T(8,128)} %qold_hbm.1, f32[6,192,128]{2,1,0:T(8,128)} %guess_hbm.1, f32[1,128]{1,0:T(1,128)} %get-tuple-element.10.cos_hbm, ...), custom_call_target="tpu_custom_call" | custom-call | tf_op jit(solution)/shard_map/section/pallas_call | solution.py:881
  104.2 3.5 %move.1 = (f32[3,6,24,1024]{3,2,1,0:T(8,128)}, f32[3,6,192,128]{3,2,1,0:T(8,128)}, f32[6,192,128]{2,1,0:T(8,128)}) custom-call(f32[3,6,24,1024]{3,2,1,0:T(8,128)} %get-tuple-element.6.refs_0_, f32[3,6,192,128]{3,2,1,0:T(8,128)} %get-tuple-element.7.refs_1_, f32[6,192,128]{2,1,0:T(8,128)} %get-tuple-element.8.refs_2_), custom_call_target="tpu_custom_call" | custom-call | tf_op jit(solution)/shard_map/move/pallas_call | solution.py:882

commit v5 on v4

--- a/solution.py
+++ b/solution.py
@@ -43,6 +43,7 @@
     inv_coarse = np.concatenate([np.cos(alpha), np.sin(alpha)])
     inv_fine = (2.0 * section_weight * scale) * np.stack([np.cos(beta), -np.sin(beta)])
     wave_y = 2.0 * np.pi / width_y * mode[None, :]
+    wave_y = np.concatenate([wave_y, np.cos(fraction * wave_y), np.sin(fraction * wave_y)])
     m = np.arange(depth_z)
     signed = np.where(m < depth_z // 2, m, m - depth_z)
     wave_z = (2.0 * np.pi / depth_z * signed)[:, None]
@@ -88,8 +89,6 @@
     vel_hbm,
     qold_hbm,
     guess_hbm,
-    cos_hbm,
-    sin_hbm,
     fcoarse_hbm,
     ffine_hbm,
     icoarse_hbm,
@@ -109,7 +108,6 @@
     wavey,
     wavez,
     zmat,
-    edge,
     qold,
     f_hi,
     f_lo,
@@ -146,7 +144,7 @@
     right = lax.rem(gx + 1, slabs)
     left = lax.rem(gx + slabs - 1, slabs)
     relayed = slabs == 16
-    near = 384
+    near = 256
     planes = 6
     rows = 24
     width = 1024
@@ -170,8 +168,6 @@
         (ffine_hbm, ffine.at[0]),
         (guess_hbm, guess.at[pl.ds(1, planes)]),
         (wavey_hbm, wavey),
-        (cos_hbm, edge.at[0]),
-        (sin_hbm, edge.at[1]),
         (zmat_hbm, zmat),
         (wavez_hbm, wavez),
         (icoarse_hbm, icoarse),
@@ -179,7 +175,7 @@
         (qold_hbm, qold),
     ]
     loads = [pltpu.make_async_copy(s, d, load_sem.at[i]) for i, (s, d) in enumerate(loads)]
-    for i in (1, 2, 0, 3, 4, 5, 6, 7, 8, 9, 10, 11):
+    for i in (1, 2, 0, 3, 4, 5, 6, 7, 8, 9):
         loads[i].start()
 
     barrier = pltpu.get_barrier_semaphore()
@@ -488,7 +484,7 @@
         lax.fori_loop(0, 4, send_w, 0)
         fwd_own(spec_w, got_w, kind, at, count).start()
 
-    for i in (5, 6, 7, 8, 9, 10):
+    for i in (5, 6, 7, 8):
         loads[i].wait()
     own_ky = wavey[0:1, own_cols(me)]
     recip[...] = 1.0 / (2.0 + own_ky * own_ky + wavez[...] * wavez[...])
@@ -513,8 +509,26 @@
         lines = table[0:16, :].astype(F32)
         table[0:16, :] = jnp.where(top, lines * 0.5, lines).astype(BF16)
 
-    cosine = edge[0]
-    sine = edge[1]
+    own = own_cols(me)
+    coarse = shift // half
+    fine = lax.rem(shift, half)
+    real_lane = lax.broadcasted_iota(jnp.int32, (1, lanes), 1) < half
+
+    def row_of(lines, row):
+        there = lax.broadcasted_iota(jnp.int32, lines.shape, 0) == row
+        return jnp.sum(jnp.where(there, lines, 0.0), axis=0, keepdims=True)
+
+    first_row = row_of(ffine[0, :, own], fine)
+    second_row = row_of(ffine[1, :, own], fine)
+    unit = math.sqrt(width)
+    cos_b = unit * jnp.where(real_lane, first_row, -second_row)
+    sin_b = -unit * jnp.where(real_lane, second_row, first_row)
+    cos_c, sin_c = wavey[1:2, own], wavey[2:3, own]
+    cos_b, sin_b = cos_b * cos_c - sin_b * sin_c, sin_b * cos_c + cos_b * sin_c
+    cos_c = row_of(fcoarse[0 : width // half, own], coarse)
+    sin_c = row_of(fcoarse[width // half : 2 * width // half, own], coarse)
+    cosine = cos_b * cos_c - sin_b * sin_c
+    sine = sin_b * cos_c + cos_b * sin_c
 
     def rotate_ends(lower, upper):
         @pl.when(gx == 0)
@@ -629,7 +643,7 @@
 
     for j in (1, 2, 3, 4):
         sweep_again(j)
-    loads[11].wait()
+    loads[9].wait()
 
     def inv_copy(pair, c, dest):
         at = pair * 6 + c * 2
@@ -739,15 +753,15 @@
         left_side[rows_c : 2 * rows_c, :] = low
 
         def cells(k, inner):
-            cols = pl.ds(pl.multiple_of(k * 256, 256), 256)
+            cols = pl.ds(pl.multiple_of(k * 512, 512), 512)
             both = mm(left_side[0 : 2 * rows_c, :], f_hi[:, cols])
             out = both[:rows_c] + both[rows_c:] + mm(left_side[0:rows_c, :], f_lo[:, cols])
             spec_u[pl.ds(at, 2), :, cols] = (
-                ghost[c, pl.ds(3 + 2 * pair, 2), :, cols] + out.reshape(2, rows, 256)
+                ghost[c, pl.ds(3 + 2 * pair, 2), :, cols] + out.reshape(2, rows, 512)
             )
             return inner
 
-        lax.fori_loop(0, 4, cells, 0)
+        lax.fori_loop(0, 2, cells, 0)
         result(c, pair, 2 + pair * 3 + c).start()
         return carry
 
@@ -813,18 +827,13 @@
     half = width // (2 * GROUPS)
     planes, rows = vel.shape[1], vel.shape[2]
     consts = tables(width, depth)
-    modes = lax.axis_index("yz") * half + jnp.arange(2 * half, dtype=jnp.int32) % half
-    angle = (2.0 * math.pi / width) * (
-        (modes * shear_shift[0] % width).astype(F32) + fraction * modes.astype(F32)
-    )
-    edge = (jnp.cos(angle)[None], jnp.sin(angle)[None])
     any_spec = pl.BlockSpec(memory_space=pl.ANY)
     vmem = lambda *shape: pltpu.VMEM(shape, F32)
     wide = lambda n: pltpu.VMEM((n, depth, 2 * half), F32)
     flat = 3 * planes * rows
     scratch = [
         vmem(3, planes + 6, rows, width),
-        vmem(3, 3, rows, width - 384),
+        vmem(3, 3, rows, width - 256),
         vmem(*consts[0].shape),
         vmem(2, *consts[1].shape),
         vmem(*consts[2].shape),
@@ -832,7 +841,6 @@
         vmem(*consts[4].shape),
         vmem(*consts[5].shape),
         pltpu.VMEM(consts[6].shape, BF16),
-        vmem(2, 1, 2 * half),
         vmem(3, planes, depth, 2 * half),
         pltpu.VMEM((width, width), BF16),
         pltpu.VMEM((width, width), BF16),
@@ -854,7 +862,7 @@
         wide(planes + 2),
         wide(3 * planes),
         vmem(3 * planes, rows, width),
-        pltpu.SemaphoreType.DMA((12,)),
+        pltpu.SemaphoreType.DMA((10,)),
         pltpu.SemaphoreType.DMA((10,)),
         pltpu.SemaphoreType.DMA((10,)),
         pltpu.SemaphoreType.DMA((7, GROUPS)),
@@ -870,7 +878,7 @@
             jax.ShapeDtypeStruct(q_old.shape, F32),
             jax.ShapeDtypeStruct(pressure_guess.shape, F32),
         ),
-        in_specs=[pl.BlockSpec(memory_space=pltpu.SMEM)] + [any_spec] * 12,
+        in_specs=[pl.BlockSpec(memory_space=pltpu.SMEM)] + [any_spec] * 10,
         out_specs=(any_spec, any_spec, any_spec),
         scratch_shapes=scratch,
         compiler_params=pltpu.CompilerParams(
@@ -878,7 +886,7 @@
         ),
         name="section",
     )
-    out = call(shear_shift, vel, q_old, pressure_guess, *edge, *consts)
+    out = call(shear_shift, vel, q_old, pressure_guess, *consts)
     return pl.pallas_call(
         move,
         out_shape=tuple(jax.ShapeDtypeStruct(v.shape, F32) for v in out),

time: 108 us -> 106 us (0.981); the launches traced: 108 us -> 104 us
  Pallas kernels: 106 us -> 103 us
    pallas_call x1, Pallas kernels: 102 us -> 99.5 us  [local(): out = call(shear_shift, vel, q_old, pressure_guess, *consts)]
where the time goes in v5:
time: 106 us; the launch traced here: 104 us
  Pallas kernels  103 us (97%)
  between operations  1.29 us (1%)
    pallas_call x1, Pallas kernels, local(): out = call(shear_shift, vel, q_old, pressure_guess, *consts)  99.5 us
    pallas_call x1, Pallas kernels, local(): pl.pallas_call(move, out_shape=tuple((jax.ShapeDtypeStruct(v.shape, F32)...  3.47 us

profile of v5, /device:TPU:0, one launch (start us, length us, event | category | flops | bytes accessed | tf_op | source)
XLA Modules:
  0.0 104.2 jit_solution(16742011057218979040)
XLA Ops:
  1.3 99.5 %section.1 = (f32[3,6,24,1024]{3,2,1,0:T(8,128)}, f32[3,6,192,128]{3,2,1,0:T(8,128)}, f32[6,192,128]{2,1,0:T(8,128)}) custom-call(s32[1]{0:T(128)S(6)} %copy.14.shift_ref, f32[3,6,24,1024]{3,2,1,0:T(8,128)} %vel_hbm.1, f32[3,6,192,128]{3,2,1,0:T(8,128)} %qold_hbm.1, f32[6,192,128]{2,1,0:T(8,128)} %guess_hbm.1, f32[32,1024]{1,0:T(8,128)} %constant.14.clone.fcoarse_hbm, ...), custom_call_target="tpu_custom_call" | custom-call | tf_op jit(solution)/shard_map/section/pallas_call | solution.py:889
  100.8 3.5 %move.1 = (f32[3,6,24,1024]{3,2,1,0:T(8,128)}, f32[3,6,192,128]{3,2,1,0:T(8,128)}, f32[6,192,128]{2,1,0:T(8,128)}) custom-call(f32[3,6,24,1024]{3,2,1,0:T(8,128)} %get-tuple-element.6.refs_0_, f32[3,6,192,128]{3,2,1,0:T(8,128)} %get-tuple-element.7.refs_1_, f32[6,192,128]{2,1,0:T(8,128)} %get-tuple-element.8.refs_2_), custom_call_target="tpu_custom_call" | custom-call | tf_op jit(solution)/shard_map/move/pallas_call | solution.py:890

commit v6 on v5

--- a/solution.py
+++ b/solution.py
@@ -724,7 +724,11 @@
     results += [result(c, pair, 2 + pair * 3 + c) for pair in range(3) for c in range(3)]
 
     def sent_u(d, carry):
-        fwd_copy(spec_u, got_u, 0, peer(d), 0, 18).wait_send()
+        dest = peer(d)
+        fwd_copy(spec_u, got_u, 0, dest, 0, 18).wait_send()
+        fwd_copy(spec_c, got_c, 1, dest, 0, 18).wait_send()
+        for kind, at, count in w_parts:
+            fwd_copy(spec_w, got_w, kind, dest, at, count).wait_send()
         return carry
 
     lax.fori_loop(1, GROUPS, sent_u, 0)
@@ -769,9 +773,6 @@
 
     def drain(d, carry):
         dest = peer(d)
-        fwd_copy(spec_c, got_c, 1, dest, 0, 18).wait_send()
-        for kind, at, count in w_parts:
-            fwd_copy(spec_w, got_w, kind, dest, at, count).wait_send()
         for pair in range(3):
             for c in range(3):
                 inv_copy(pair, c, dest).wait_send()

time: 106 us -> 106 us (level)
  no operation moved by 1% of the time
where the time goes in v6:
time: 106 us; the launch traced here: 104 us
  Pallas kernels  103 us (97%)
  between operations  1.29 us (1%)
    pallas_call x1, Pallas kernels, local(): out = call(shear_shift, vel, q_old, pressure_guess, *consts)  99.5 us
    pallas_call x1, Pallas kernels, local(): pl.pallas_call(move, out_shape=tuple((jax.ShapeDtypeStruct(v.shape, F32)...  3.47 us

profile of v6, /device:TPU:0, one launch (start us, length us, event | category | flops | bytes accessed | tf_op | source)
XLA Modules:
  0.0 104.2 jit_solution(7302954090904193377)
XLA Ops:
  1.3 99.5 %section.1 = (f32[3,6,24,1024]{3,2,1,0:T(8,128)}, f32[3,6,192,128]{3,2,1,0:T(8,128)}, f32[6,192,128]{2,1,0:T(8,128)}) custom-call(s32[1]{0:T(128)S(6)} %copy.14.shift_ref, f32[3,6,24,1024]{3,2,1,0:T(8,128)} %vel_hbm.1, f32[3,6,192,128]{3,2,1,0:T(8,128)} %qold_hbm.1, f32[6,192,128]{2,1,0:T(8,128)} %guess_hbm.1, f32[32,1024]{1,0:T(8,128)} %constant.14.clone.fcoarse_hbm, ...), custom_call_target="tpu_custom_call" | custom-call | tf_op jit(solution)/shard_map/section/pallas_call | solution.py:890
  100.8 3.5 %move.1 = (f32[3,6,24,1024]{3,2,1,0:T(8,128)}, f32[3,6,192,128]{3,2,1,0:T(8,128)}, f32[6,192,128]{2,1,0:T(8,128)}) custom-call(f32[3,6,24,1024]{3,2,1,0:T(8,128)} %get-tuple-element.6.refs_0_, f32[3,6,192,128]{3,2,1,0:T(8,128)} %get-tuple-element.7.refs_1_, f32[6,192,128]{2,1,0:T(8,128)} %get-tuple-element.8.refs_2_), custom_call_target="tpu_custom_call" | custom-call | tf_op jit(solution)/shard_map/move/pallas_call | solution.py:891
